TPU v7x, 512 devices: a whole 4x8x8 slice. The times are simulated.
512 devices in a mesh: dp: 4 (over x), ep: 128 (over y, z, core).
Axes of the slice: x: 4, y: 8, z: 8, core: 2. Of those that a mesh axis runs over, the one named last changes fastest.
Arguments:
- tokens: bfloat16 [4096, 1024], P(('dp', 'ep')), may hold values from -6 to 6
- expert_ids: int32 [4096, 8], P(('dp', 'ep')), may hold values from 0 to 127, all different within a row; in each aligned block of 8 rows (0 to 7, 8 to 15, ...) no two rows name the same one
- gate_quant: int32 [4096, 8], P(('dp', 'ep')), may hold values from 1 to 1024
- bucket_ids: int32 [4096], P(('dp', 'ep')), may hold values from 0 to 15
- bucket_counts: int32 [16], replicated, may hold values from 0 to 512
- gate_weight: bfloat16 [128, 1024, 384], P('ep', 'dp'), may hold values from -0.1875 to 0.1875
- up_weight: bfloat16 [128, 1024, 384], P('ep', 'dp'), may hold values from -0.1875 to 0.1875
- down_weight: bfloat16 [128, 384, 1024], P('ep', 'dp'), may hold values from -0.3125 to 0.3125
- cotangent: bfloat16 [4096, 1024], P(('dp', 'ep')), may hold values from -6 to 6
Outputs:
- layer_out: bfloat16 [4096, 1024], P(('dp', 'ep'))
- token_grad: bfloat16 [4096, 1024], P(('dp', 'ep'))
- gate_grad: float32 [128, 1024, 384], P('ep', 'dp')
- up_grad: float32 [128, 1024, 384], P('ep', 'dp')
- down_grad: float32 [128, 384, 1024], P('ep', 'dp')
Inputs may be any that keep to these rules, and one draw needn't show every extreme that they name: `expert_ids`: each row names 8 different experts. Among the 8 rows of one device no expert is named by more than 1 row, and in every draw some expert is named by exactly 1 row of some device.
All inputs are finite; a program needn't handle non-finite values.
Results may differ from a plain program's by a relative error of at most 0.0085.
Values may be sent and summed in bfloat16 or wider, within the bound.
A program may use at most 64 MiB of HBM per device.

v0:
```python
import jax
import jax.numpy as jnp
from jax import lax
from jax.sharding import PartitionSpec as P


def sent_together(arrays, axis, dim, along):
    ends, at = ([], 0)
    for a in arrays[:-1]:
        at += a.shape[along]
        ends.append(at)
    both = jnp.concatenate(arrays, axis=along)
    return tuple(jnp.split(lax.all_gather(both, axis, axis=dim, tiled=True), ends, axis=along))


def side_by_side(arrays, axis, split_dim, concat_dim, along):
    both = jnp.concatenate(arrays, axis=along)
    filled, at, outs = (
        lax.all_to_all(both, axis, split_axis=split_dim, concat_axis=concat_dim, tiled=True),
        0,
        [],
    )
    for a in arrays:
        outs.append(lax.slice_in_dim(filled, at, at + a.shape[along], axis=along))
        at += a.shape[along]
    return tuple(outs)


def sent_together_2(arrays, axis, dim, along):
    ends, at = ([], 0)
    for a in arrays[:-1]:
        at += a.shape[along]
        ends.append(at)
    both = jnp.concatenate(arrays, axis=along)
    return tuple(
        jnp.split(lax.psum_scatter(both, axis, scatter_dimension=dim, tiled=True), ends, axis=along)
    )


def silu_parts(pre_gate):
    sigmoid_val = jax.nn.sigmoid(pre_gate)
    return (pre_gate * sigmoid_val, sigmoid_val * (1.0 + pre_gate * (1.0 - sigmoid_val)))


def contract_rows(left_rows, right_rows):
    return lax.dot_general(
        left_rows, right_rows, (((0,), (0,)), ((), ())), preferred_element_type=jnp.float32
    )


def contract_cols(left_rows, right_rows):
    return lax.dot_general(
        left_rows, right_rows, (((1,), (1,)), ((), ())), preferred_element_type=jnp.float32
    )


def expert_forward(rows_in, gate_full, up_full, down_full):
    pre_gate = jnp.dot(rows_in, gate_full, preferred_element_type=jnp.float32)
    pre_up = jnp.dot(rows_in, up_full, preferred_element_type=jnp.float32)
    activation, derivative = silu_parts(pre_gate)
    hidden = (activation * pre_up).astype(jnp.bfloat16)
    expert_out = jnp.dot(hidden, down_full, preferred_element_type=jnp.float32).astype(jnp.bfloat16)
    return (expert_out, (pre_up, activation, derivative, hidden))


def expert_backward(rows_in, scaled, saved, gate_full, up_full, down_full):
    pre_up, activation, derivative, hidden = saved
    hidden_grad = contract_cols(scaled, down_full)
    gate_pre = (hidden_grad * pre_up * derivative).astype(jnp.bfloat16)
    up_pre = (hidden_grad * activation).astype(jnp.bfloat16)
    slot_grad = (contract_cols(gate_pre, gate_full) + contract_cols(up_pre, up_full)).astype(
        jnp.bfloat16
    )
    return (
        slot_grad,
        contract_rows(rows_in, gate_pre),
        contract_rows(rows_in, up_pre),
        contract_rows(hidden, scaled),
    )


def slot_table(flat_ids, experts, slot_cap):
    total_pairs = flat_ids.shape[0]
    onehot = (flat_ids[:, None] == jnp.arange(experts, dtype=jnp.int32)[None, :]).astype(jnp.int32)
    before = jnp.cumsum(onehot, axis=0) - onehot
    position = jnp.sum(before * onehot, axis=1)
    slot_of = flat_ids * slot_cap + position
    lookup = jnp.full((experts * slot_cap,), total_pairs, jnp.int32)
    lookup = lookup.at[slot_of].set(jnp.arange(total_pairs, dtype=jnp.int32))
    return (lookup, slot_of)


def per_device(
    tokens,
    expert_ids,
    gate_quant,
    bucket_ids,
    bucket_counts,
    gate_weight,
    up_weight,
    down_weight,
    cotangent,
):
    experts = lax.axis_size("ep")
    tok_rows, top_count = expert_ids.shape
    model_width = tokens.shape[1]
    slot_cap = min(tok_rows, 2 * tok_rows * top_count // experts)
    gate_share = gate_quant.astype(jnp.float32) / 1024.0
    bucket_match = (
        bucket_ids[:, None] == jnp.arange(bucket_counts.shape[0], dtype=jnp.int32)[None, :]
    ).astype(jnp.float32)
    count_of = jnp.sum(bucket_match * bucket_counts.astype(jnp.float32)[None, :], axis=1)
    token_scale = 64.0 / (64.0 + count_of)
    flat_ids = expert_ids.reshape(-1)
    total_pairs = flat_ids.shape[0]
    lookup, slot_of = slot_table(flat_ids, experts, slot_cap)
    is_live = lookup < total_pairs
    safe_index = jnp.where(is_live, lookup, 0)
    source_row = safe_index // top_count
    send_rows = jnp.where(is_live[:, None], tokens[source_row], jnp.zeros((), jnp.bfloat16))
    send_rows = send_rows.reshape(experts, slot_cap, model_width)
    scaled_flat = (gate_share * token_scale[:, None]).reshape(-1)
    scale_slot = jnp.where(is_live, scaled_flat[safe_index], jnp.zeros((), jnp.float32))
    send_grads = (scale_slot[:, None] * cotangent[source_row].astype(jnp.float32)).astype(
        jnp.bfloat16
    )
    send_grads = send_grads.reshape(experts, slot_cap, model_width)
    gate_full, up_full, down_full = (
        *sent_together((gate_weight, up_weight), "dp", 1, 0),
        lax.all_gather(down_weight, "dp", axis=1, tiled=True),
    )
    gate_full = gate_full[0]
    up_full = up_full[0]
    down_full = down_full[0]
    recv_rows, recv_grads = side_by_side((send_rows, send_grads), "ep", 0, 0, 1)
    rows_in = recv_rows.reshape(-1, model_width)
    scaled = recv_grads.reshape(-1, model_width)
    expert_out, saved = expert_forward(rows_in, gate_full, up_full, down_full)
    slot_grad, grad_gate, grad_up, grad_down = expert_backward(
        rows_in, scaled, saved, gate_full, up_full, down_full
    )
    out_back, grad_back = side_by_side(
        (
            expert_out.reshape(experts, slot_cap, model_width),
            slot_grad.reshape(experts, slot_cap, model_width),
        ),
        "ep",
        0,
        0,
        1,
    )
    out_pairs = out_back.reshape(experts * slot_cap, model_width)[slot_of].astype(jnp.float32)
    out_pairs = out_pairs.reshape(tok_rows, top_count, model_width)
    layer_out = jnp.sum(gate_share[:, :, None] * out_pairs, axis=1).astype(jnp.bfloat16)
    grad_pairs = grad_back.reshape(experts * slot_cap, model_width)[slot_of].astype(jnp.float32)
    token_grad = jnp.sum(grad_pairs.reshape(tok_rows, top_count, model_width), axis=1).astype(
        jnp.bfloat16
    )
    summed = (
        *tuple(
            (
                part.astype(jnp.float32)
                for part in sent_together_2(
                    (grad_gate[None].astype(jnp.bfloat16), grad_up[None].astype(jnp.bfloat16)),
                    "dp",
                    1,
                    0,
                )
            )
        ),
        lax.psum_scatter(
            grad_down[None].astype(jnp.bfloat16), "dp", scatter_dimension=1, tiled=True
        ).astype(jnp.float32),
    )
    return (layer_out, token_grad, summed[0], summed[1], summed[2])


def solution(mesh):
    placed = (
        P(("dp", "ep"), None),
        P(("dp", "ep"), None),
        P(("dp", "ep"), None),
        P(("dp", "ep")),
        P(),
        P("ep", "dp", None),
        P("ep", "dp", None),
        P("ep", "dp", None),
        P(("dp", "ep"), None),
    )
    return jax.shard_map(
        per_device,
        mesh=mesh,
        in_specs=placed,
        out_specs=(
            P(("dp", "ep"), None),
            P(("dp", "ep"), None),
            P("ep", "dp", None),
            P("ep", "dp", None),
            P("ep", "dp", None),
        ),
        check_vma=False,
    )
```

profile of v0, /device:TPU:1, one launch (start us, length us, event | category | flops | bytes accessed | tf_op | source)
XLA Modules:
  0.0 129.8 jit_solution(1899097009334134533)
XLA Ops:
  7.2 1.8 %pad_maximum_fusion.3 = bf16[2,256,384]{2,1,0:T(8,128)(2,1)} fusion(bf16[1,256,384]{2,1,0:T(8,128)(2,1)} %param.15, bf16[1,256,384]{2,1,0:T(8,128)(2,1)} %param.14), kind=kLoop, calls=%fused_computation.30 | loop fusion | flops 196608 | bytes 786432 | tf_op jit(solution)/shard_map/concatenate | solution.py:12
  9.1 0.8 eq.28
  9.8 0.8 reshape.134
  11.3 0.8 select_reduce_fusion.1
  12.1 0.8 convert_multiply_fusion.3
  13.3 0.8 scatter_custom_fusion
  14.2 1.2 gather_fusion.1
  15.4 0.9 gather_fusion.2
  16.3 0.9 gather_fusion
  17.4 1.3 %copy.24 = bf16[128,2,1024]{2,1,0:T(2,128)(2,1)} copy(bf16[128,2,1024]{2,0,1:T(8,128)(2,1)S(1)} %pad_maximum_fusion.1) | data formatting | bytes 1048576 | tf_op jit(solution)/shard_map/concatenate | solution.py:17
  18.8 18.4 %all-to-all-start = ((bf16[128,2,1024]{2,1,0:T(2,128)(2,1)}), bf16[128,2,1024]{2,1,0:T(2,128)(2,1)S(1)}, u32[]{:S(2)}, u32[]{:S(2)}) async-start(bf16[128,2,1024]{2,1,0:T(2,128)(2,1)} %copy.24), calls=%async_computation | async-start | bytes 1048576 | tf_op jit(solution)/shard_map/all_to_all | solution.py:19
  37.3 16.6 %all_gather.7 = bf16[1,384,1024]{2,1,0:T(8,128)(2,1)S(1)} all-gather(bf16[1,96,1024]{2,1,0:T(8,128)(2,1)S(1)} %copy-done.3), channel_id=1, replica_groups=mesh['dp'=4,'ep'=128] {'dp'}, dimensions={1}, use_global_device_ids=true | all-gather | bytes 983040 | tf_op jit(solution)/shard_map/all_gather | solution.py:130
  53.8 2.8 %all-to-all-done = bf16[128,2,1024]{2,1,0:T(2,128)(2,1)S(1)} async-done(((bf16[128,2,1024]{2,1,0:T(2,128)(2,1)}), bf16[128,2,1024]{2,1,0:T(2,128)(2,1)S(1)}, u32[]{:S(2)}, u32[]{:S(2)}) %all-to-all-start) | async-done | bytes 524320 | tf_op jit(solution)/shard_map/all_to_all | solution.py:19
  57.8 1.4 %fusion.10 = f32[128,384]{1,0:T(8,128)S(1)} fusion(bf16[128,1024]{1,0:T(8,128)(2,1)S(1)} %bitcast.67, bf16[2,1024,384]{2,1,0:T(8,128)(2,1)} %all-gather.2.cloned.1.call-done), kind=kOutput, calls=%fused_computation.24 | convolution fusion | flops 100663296 | bytes 1245184 | tf_op jit(solution)/shard_map/dot_general | solution.py:58
  59.3 1.4 %multiply_convert_fusion.2 = (bf16[128,384]{1,0:T(8,128)(2,1)S(1)}, bf16[128,384]{1,0:T(8,128)(2,1)S(1)}, bf16[128,384]{1,0:T(8,128)(2,1)S(1)}) fusion(f32[128,384]{1,0:T(8,128)S(1)} %fusion.10, f32[128,384]{1,0:T(8,128)S(1)} %fusion.6, bf16[128,1024]{1,0:T(8,128)(2,1)S(1)} %bitcast.68, bf16[2,1024,384]{2,1,0:T(8,128)(2,1)} %all-gather.2.cloned.1.call-done), kind=kOutput, calls=%fused_computation.42 | convolution fusion | flops 101400576 | bytes 1736704 | tf_op jit(solution)/shard_map/dot_general | solution.py:59
  60.7 1.3 fusion.2
  62.9 1.3 %pad_maximum_fusion = bf16[2,1024,384]{2,1,0:T(8,128)(2,1)} fusion(bf16[1,1024,384]{2,1,0:T(8,128)(2,1)S(1)} %fusion.1, bf16[1,1024,384]{2,1,0:T(8,128)(2,1)S(1)} %fusion), kind=kLoop, calls=%fused_computation.6 | loop fusion | flops 786432 | bytes 3145728 | tf_op jit(solution)/shard_map/concatenate | solution.py:34
  64.5 1.1 copy-done.2
  66.4 1.3 %copy.27 = bf16[128,2,1024]{2,1,0:T(2,128)(2,1)} copy(bf16[128,2,1024]{2,0,1:T(8,128)(2,1)S(1)} %pad_maximum_fusion.2) | data formatting | bytes 1048576 | tf_op jit(solution)/shard_map/concatenate | solution.py:17
  67.8 12.6 %all-to-all-start.1 = ((bf16[128,2,1024]{2,1,0:T(2,128)(2,1)}), bf16[128,2,1024]{2,1,0:T(2,128)(2,1)S(1)}, u32[]{:S(2)}, u32[]{:S(2)}) async-start(bf16[128,2,1024]{2,1,0:T(2,128)(2,1)} %copy.27), calls=%async_computation.1 | async-start | bytes 1048576 | tf_op jit(solution)/shard_map/all_to_all | solution.py:19
  80.4 19.4 %all-to-all-done.1 = bf16[128,2,1024]{2,1,0:T(2,128)(2,1)S(1)} async-done(((bf16[128,2,1024]{2,1,0:T(2,128)(2,1)}), bf16[128,2,1024]{2,1,0:T(2,128)(2,1)S(1)}, u32[]{:S(2)}, u32[]{:S(2)}) %all-to-all-start.1) | async-done | bytes 524320 | tf_op jit(solution)/shard_map/all_to_all | solution.py:19
  103.6 1.7 %convert_element_type.110 = f32[1,96,1024]{2,1,0:T(8,128)} convert(bf16[1,96,1024]{2,1,0:T(8,128)(2,1)} %reduce-scatter.5.cloned.1.call-done) | non-fusion elementwise | flops 98304 | bytes 589824 | tf_op jit(solution)/shard_map/convert_element_type | solution.py:173
  105.3 16.0 %reduce-scatter.3.cloned.1.call-done = bf16[2,256,384]{2,1,0:T(8,128)(2,1)} async-done(((bf16[2,1024,384]{2,1,0:T(8,128)(2,1)}), bf16[2,256,384]{2,1,0:T(8,128)(2,1)}) %reduce-scatter.3.cloned.1.call-update) | async-done | bytes 393232 | tf_op jit(solution)/shard_map/reduce_scatter | solution.py:36
  121.3 1.9 %slice_convert_fusion = (f32[1,256,384]{2,1,0:T(8,128)}, f32[1,256,384]{2,1,0:T(8,128)}) fusion(bf16[2,256,384]{2,1,0:T(8,128)(2,1)} %reduce-scatter.3.cloned.1.call-done), kind=kLoop, calls=%fused_computation.38 | loop fusion | flops 196608 | bytes 1179648 | tf_op jit(solution)/shard_map/convert_element_type | solution.py:162
  (47 shorter events, 8.4 us)
Async XLA Ops:
  7.2 8.2 %copy-start = (bf16[8,1024]{1,0:T(8,128)(2,1)S(1)}, bf16[8,1024]{1,0:T(8,128)(2,1)}, u32[]{:S(2)}) copy-start(bf16[8,1024]{1,0:T(8,128)(2,1)} %param.17) | copy-start | bytes 49156
  7.2 50.7 %all-gather.2.cloned.1.call-start = ((), (), s32[]{:S(2)}) async-start(), calls=%async_computation.4 | async-start | bytes 1966080 | tf_op jit(solution)/shard_map/all_gather | solution.py:13
  9.1 7.2 %copy-start.1 = (bf16[8,1024]{1,0:T(8,128)(2,1)S(1)}, bf16[8,1024]{1,0:T(8,128)(2,1)}, u32[]{:S(2)}) copy-start(bf16[8,1024]{1,0:T(8,128)(2,1)} %param.9) | copy-start | bytes 49156
  17.4 19.9 %copy-start.3 = (bf16[1,96,1024]{2,1,0:T(8,128)(2,1)S(1)}, bf16[1,96,1024]{2,1,0:T(8,128)(2,1)}, u32[]{:S(2)}) copy-start(bf16[1,96,1024]{2,1,0:T(8,128)(2,1)} %param.16) | copy-start | bytes 589828
  18.8 37.8 %all-to-all-start = ((bf16[128,2,1024]{2,1,0:T(2,128)(2,1)}), bf16[128,2,1024]{2,1,0:T(2,128)(2,1)S(1)}, u32[]{:S(2)}, u32[]{:S(2)}) async-start(bf16[128,2,1024]{2,1,0:T(2,128)(2,1)} %copy.24), calls=%async_computation | async-start | bytes 1048576 | tf_op jit(solution)/shard_map/all_to_all | solution.py:19
  37.2 66.4 %reduce-scatter.5.cloned.1.call-start = ((), (), s32[]{:S(2)}) async-start(), calls=%async_computation.6 | async-start | bytes 983040 | tf_op jit(solution)/shard_map/reduce_scatter | solution.py:171
  62.0 59.3 %reduce-scatter.3.cloned.1.call-start = ((), (), s32[]{:S(2)}) async-start(), calls=%async_computation.5 | async-start | bytes 1966080 | tf_op jit(solution)/shard_map/reduce_scatter | solution.py:36
  64.2 1.4 %copy-start.2 = (bf16[2,1024,384]{2,1,0:T(8,128)(2,1)S(1)}, bf16[2,1024,384]{2,1,0:T(8,128)(2,1)}, u32[]{:S(2)}) copy-start(bf16[2,1024,384]{2,1,0:T(8,128)(2,1)} %all-gather.2.cloned.1.call-done) | copy-start | bytes 4718596
  67.8 32.1 %all-to-all-start.1 = ((bf16[128,2,1024]{2,1,0:T(2,128)(2,1)}), bf16[128,2,1024]{2,1,0:T(2,128)(2,1)S(1)}, u32[]{:S(2)}, u32[]{:S(2)}) async-start(bf16[128,2,1024]{2,1,0:T(2,128)(2,1)} %copy.27), calls=%async_computation.1 | async-start | bytes 1048576 | tf_op jit(solution)/shard_map/all_to_all | solution.py:19
Sparse Core Ops, SparseCore 0:
  10.7 41.4 all-gather.1
  62.1 24.3 reduce-scatter.4
  89.4 31.8 reduce-scatter.2
where the time goes:
time: 130 us
  waiting for transfers between devices  38.3 us (29%)
  starting transfers between devices  31.2 us (24%)
  blocking collectives  16.6 us (13%)
  between operations  14 us (11%)
  local copies, waits for them, and re-layouts  12.2 us (9%)
  other arithmetic  11.2 us (9%)
  matrix products  6.35 us (5%)
    all_to_all x2, starting transfers between devices, side_by_side(): lax.all_to_all(both, axis, split_axis=split_dim, concat_axis=concat_dim,...  31 us
    all_to_all x2, waiting for transfers between devices, side_by_side(): lax.all_to_all(both, axis, split_axis=split_dim, concat_axis=concat_dim,...  22.2 us
    all_gather x1, blocking collectives, per_device(): lax.all_gather(down_weight, 'dp', axis=1, tiled=True)  16.6 us
    reduce_scatter x1, waiting for transfers between devices, sent_together_2(): lax.psum_scatter(both, axis, scatter_dimension=dim, tiled=True)  16 us
    concatenate x2, local copies, waits for them, and re-layouts, side_by_side(): both = jnp.concatenate(arrays, axis=along)  2.66 us
  transfers between devices with their start and end apart: 5, of which 3 were waited for; matrix products, arithmetic and copies ran while one was open for 16% of the time, Pallas kernels for 0%

commit v1 on v0

v1 whole, which is shorter than its diff:
```python
import jax
import jax.numpy as jnp
from jax import lax
from jax.experimental import pallas as pl
from jax.experimental.pallas import tpu as pltpu
from jax.sharding import PartitionSpec as P

MESH = pl.DeviceIdType.MESH
BF = jnp.bfloat16
F32 = jnp.float32
NX, NY, NZ, NC = 4, 8, 8, 2
NE = NY * NZ * NC
LANES = 128


def dot(a, b, ca=1, cb=0):
    return lax.dot_general(a, b, (((ca,), (cb,)), ((), ())), preferred_element_type=F32)


def rows(ref, start, size):
    return ref.at[pl.ds(pl.multiple_of(start, 16), size)]


def kernel(
    bucket_ids,
    bucket_counts,
    tokens,
    cotangent,
    expert_ids,
    gate_quant,
    gate_own,
    up_own,
    down_own,
    layer_out,
    token_grad,
    gate_grad,
    up_grad,
    down_grad,
    gate_full,
    up_full,
    down_full,
    send,
    recv,
    back_send,
    back_recv,
    spread,
    rows_in,
    scaled,
    part_gate,
    part_up,
    part_down,
    hop_gate,
    hop_up,
    hop_down,
    fwd_gate,
    fwd_up,
    fwd_down,
    fin_gate,
    fin_up,
    fin_down,
    step_sem,
    ag_send,
    ag_recv,
    rs_send,
    rs_recv,
    out_send,
    out_recv,
    ret_send,
    ret_recv,
):
    x = lax.axis_index("dp")
    e = lax.axis_index("ep")
    y, z, c = e // (NZ * NC), (e // NC) % NZ, e % NC
    tok_rows, top = expert_ids.shape
    width = tokens.shape[1]
    blocks = width // LANES
    slot = 2 * blocks

    def ep(yy, zz, cc):
        return (lax.rem(yy + NY, NY) * NZ + lax.rem(zz + NZ, NZ)) * NC + lax.rem(cc, NC)

    right, left, across = lax.rem(x + 1, NX), lax.rem(x + NX - 1, NX), lax.rem(x + 2, NX)
    y_near = [ep(y + d, z, c) for d in (1, -1)]
    z_near = [ep(y, z + d, c + k) for d in (1, -1) for k in (0, 1)]
    mate = ep(y, z, c + 1)

    barrier = pltpu.get_barrier_semaphore()
    for xx in (right, left):
        pl.semaphore_signal(barrier, inc=1, device_id=(xx, e), device_id_type=MESH)
    for d in (*y_near, *z_near, mate):
        pl.semaphore_signal(barrier, inc=1, device_id=(x, d), device_id_type=MESH)

    lane = lax.broadcasted_iota(jnp.int32, (tok_rows, NE), 1)
    hit = jnp.zeros((tok_rows, NE), F32)
    share = jnp.zeros((tok_rows, NE), F32)
    for k in range(top):
        here = lane == expert_ids[:, k : k + 1]
        hit = hit + jnp.where(here, 1.0, 0.0)
        share = share + jnp.where(here, gate_quant[:, k : k + 1].astype(F32), 0.0)
    share = share / 1024.0
    row = lax.broadcasted_iota(jnp.int32, (tok_rows, NE), 0)
    count = jnp.zeros((tok_rows, NE), jnp.int32)
    for t in range(tok_rows):
        count = jnp.where(row == t, bucket_counts[bucket_ids[t]], count)
    scale = share * (64.0 / (64.0 + count.astype(F32)))
    scale_col = jnp.sum(jnp.transpose(scale), axis=1, keepdims=True)
    pick = hit.astype(BF)
    picked = dot(pick, tokens[...], 0, 0)
    for j in range(blocks):
        spread[pl.ds(j, NE, stride=slot), :] = picked[:, j * LANES : (j + 1) * LANES]
    picked = dot(pick, cotangent[...], 0, 0) * scale_col
    for j in range(blocks):
        spread[pl.ds(blocks + j, NE, stride=slot), :] = picked[:, j * LANES : (j + 1) * LANES]
    send[...] = spread[...].astype(BF)

    pl.semaphore_wait(barrier, 9)

    shards = ((gate_own, gate_full), (up_own, up_full), (down_own, down_full))

    def ag_copy(src, dst, kind, i, xx):
        return pltpu.make_async_remote_copy(
            src, dst, ag_send.at[kind, i], ag_recv.at[kind, i], device_id=(xx, e), device_id_type=MESH
        )

    own_right, own_left = [], []
    for i, (own, full) in enumerate(shards):
        size = own.shape[1]
        target = rows(full, x * size, size)
        own_right.append(ag_copy(own.at[0], target, 0, i, right))
        own_left.append(ag_copy(own.at[0], target, 1, i, left))
        own_right[i].start()
        own_left[i].start()

    for s in range(NY // 2 - 1):
        for d in y_near:
            pl.semaphore_signal(step_sem.at[s], inc=1, device_id=(x, d), device_id_type=MESH)
        pl.semaphore_wait(step_sem.at[s], 2)
    for s in range(NZ // 2):
        n = NY // 2 - 1 + s
        peers = (*z_near, mate) if s == 0 else z_near
        for d in peers:
            pl.semaphore_signal(step_sem.at[n], inc=1, device_id=(x, d), device_id_type=MESH)
        pl.semaphore_wait(step_sem.at[n], len(peers))

    def exchange(src, dst, s_sem, r_sem):
        def one(i, carry):
            d = ep(y + i % NY, z + (i // NY) % NZ, c + i // (NY * NZ))
            pltpu.make_async_remote_copy(
                rows(src, d * slot, slot),
                rows(dst, e * slot, slot),
                s_sem,
                r_sem,
                device_id=(x, d),
                device_id_type=MESH,
            ).start()
            return carry

        lax.fori_loop(1, NE, one, 0)
        at = pl.multiple_of(e * slot, slot)
        dst[pl.ds(at, slot), :] = src[pl.ds(at, slot), :]

    def wait_all(ref, sem):
        part = ref.at[pl.ds(0, (NE - 1) * slot)]
        pltpu.make_async_copy(part, part, sem).wait()

    exchange(send, recv, out_send, out_recv)

    forwards = []
    for i, (own, full) in enumerate(shards):
        size = own.shape[1]
        half = size // 2
        full[pl.ds(pl.multiple_of(x * size, 16), size), :] = own[0]
        own_right[i].wait_recv()
        part = rows(full, left * size, half)
        forwards.append(ag_copy(part, part, 2, i, right))
        forwards[-1].start()
        own_left[i].wait_recv()
        part = rows(full, right * size + half, half)
        forwards.append(ag_copy(part, part, 3, i, left))
        forwards[-1].start()

    wait_all(recv, out_recv)
    spread[...] = recv[...].astype(F32)
    for j in range(blocks):
        at = slice(j * LANES, (j + 1) * LANES)
        rows_in[:, at] = spread[pl.ds(j, NE, stride=slot), :].astype(BF)
        scaled[:, at] = spread[pl.ds(blocks + j, NE, stride=slot), :].astype(BF)
    for f in forwards[:4]:
        f.wait_recv()
    pre_gate = dot(rows_in[...], gate_full[...])
    pre_up = dot(rows_in[...], up_full[...])
    sig = jax.nn.sigmoid(pre_gate)
    act = pre_gate * sig
    hidden = (act * pre_up).astype(BF)

    def rs_copy(src, dst, kind, i, xx):
        return pltpu.make_async_remote_copy(
            src, dst, rs_send.at[kind, i], rs_recv.at[kind, i], device_id=(xx, e), device_id_type=MESH
        )

    def scatter(i, part, hop, fin):
        size = part.shape[0] // NX
        half = size // 2
        copies = [
            rs_copy(rows(part, across * size, half), hop.at[0], 0, i, right),
            rs_copy(rows(part, across * size + half, half), hop.at[1], 1, i, left),
            rs_copy(rows(part, right * size + half, half), fin.at[0, 1], 2, i, right),
            rs_copy(rows(part, left * size, half), fin.at[1, 0], 3, i, left),
        ]
        for k in copies:
            k.start()
        return copies

    def pass_on(i, part, hop, fwd, fin, copies):
        size = part.shape[0] // NX
        half = size // 2
        copies[0].wait_recv()
        mine = part[pl.ds(pl.multiple_of(right * size, 16), half), :]
        fwd[0] = (hop[0].astype(F32) + mine.astype(F32)).astype(BF)
        copies.append(rs_copy(fwd.at[0], fin.at[0, 0], 4, i, right))
        copies[-1].start()
        copies[1].wait_recv()
        mine = part[pl.ds(pl.multiple_of(left * size + half, 16), half), :]
        fwd[1] = (hop[1].astype(F32) + mine.astype(F32)).astype(BF)
        copies.append(rs_copy(fwd.at[1], fin.at[1, 1], 5, i, left))
        copies[-1].start()

    part_down[...] = dot(hidden, scaled[...], 0, 0).astype(BF)
    down_copies = scatter(2, part_down, hop_down, fin_down)

    for f in forwards[4:]:
        f.wait_recv()
    hidden_grad = dot(scaled[...], down_full[...], 1, 1)
    gate_pre = (hidden_grad * pre_up * (sig * (1.0 + pre_gate * (1.0 - sig)))).astype(BF)
    up_pre = (hidden_grad * act).astype(BF)
    part_gate[...] = dot(rows_in[...], gate_pre, 0, 0).astype(BF)
    gate_copies = scatter(0, part_gate, hop_gate, fin_gate)
    part_up[...] = dot(rows_in[...], up_pre, 0, 0).astype(BF)
    up_copies = scatter(1, part_up, hop_up, fin_up)

    expert_out = dot(hidden, down_full[...])
    for j in range(blocks):
        spread[pl.ds(j, NE, stride=slot), :] = expert_out[:, j * LANES : (j + 1) * LANES]
    slot_grad = dot(gate_pre, gate_full[...], 1, 1) + dot(up_pre, up_full[...], 1, 1)
    for j in range(blocks):
        spread[pl.ds(blocks + j, NE, stride=slot), :] = slot_grad[:, j * LANES : (j + 1) * LANES]
    back_send[...] = spread[...].astype(BF)
    exchange(back_send, back_recv, ret_send, ret_recv)

    pass_on(2, part_down, hop_down, fwd_down, fin_down, down_copies)
    pass_on(0, part_gate, hop_gate, fwd_gate, fin_gate, gate_copies)
    pass_on(1, part_up, hop_up, fwd_up, fin_up, up_copies)

    def finish(part, fin, out, copies):
        size = part.shape[0] // NX
        half = size // 2
        for k in copies[2:]:
            k.wait_recv()
        for h in range(2):
            mine = part[pl.ds(pl.multiple_of(x * size + h * half, 16), half), :]
            out[0, h * half : (h + 1) * half, :] = (
                mine.astype(F32) + fin[0, h].astype(F32) + fin[1, h].astype(F32)
            )

    finish(part_down, fin_down, down_grad, down_copies)

    wait_all(back_recv, ret_recv)
    spread[...] = back_recv[...].astype(F32)
    high = share.astype(BF)
    low = (share - high.astype(F32)).astype(BF)
    for j in range(blocks):
        at = slice(j * LANES, (j + 1) * LANES)
        outs = spread[pl.ds(j, NE, stride=slot), :].astype(BF)
        layer_out[:, at] = (dot(high, outs) + dot(low, outs)).astype(BF)
        grads = spread[pl.ds(blocks + j, NE, stride=slot), :].astype(BF)
        token_grad[:, at] = dot(pick, grads).astype(BF)

    finish(part_gate, fin_gate, gate_grad, gate_copies)
    finish(part_up, fin_up, up_grad, up_copies)

    for k in (*own_right, *own_left, *forwards, *down_copies, *gate_copies, *up_copies):
        k.wait_send()
    wait_all(send, out_send)
    wait_all(back_send, ret_send)


def per_device(
    tokens,
    expert_ids,
    gate_quant,
    bucket_ids,
    bucket_counts,
    gate_weight,
    up_weight,
    down_weight,
    cotangent,
):
    width = tokens.shape[1]
    _, share, hidden = gate_weight.shape
    deep = down_weight.shape[1]
    vmem = pl.BlockSpec(memory_space=pltpu.VMEM)
    smem = pl.BlockSpec(memory_space=pltpu.SMEM)
    slots = (NE * 2 * (width // LANES), LANES)

    def pieces(lead):
        return [
            pltpu.VMEM((*lead, share // 2, hidden), BF),
            pltpu.VMEM((*lead, share // 2, hidden), BF),
            pltpu.VMEM((*lead, deep // 2, width), BF),
        ]

    full = [
        pltpu.VMEM((width, hidden), BF),
        pltpu.VMEM((width, hidden), BF),
        pltpu.VMEM((hidden, width), BF),
    ]
    dma = pltpu.SemaphoreType.DMA
    return pl.pallas_call(
        kernel,
        out_shape=[
            jax.ShapeDtypeStruct(tokens.shape, BF),
            jax.ShapeDtypeStruct(tokens.shape, BF),
            jax.ShapeDtypeStruct(gate_weight.shape, F32),
            jax.ShapeDtypeStruct(up_weight.shape, F32),
            jax.ShapeDtypeStruct(down_weight.shape, F32),
        ],
        in_specs=[smem] * 2 + [vmem] * 7,
        out_specs=[vmem] * 5,
        scratch_shapes=[
            *full,
            *[pltpu.VMEM(slots, BF)] * 4,
            pltpu.VMEM(slots, F32),
            *[pltpu.VMEM((NE, width), BF)] * 2,
            *full,
            *pieces((2,)),
            *pieces((2,)),
            *pieces((2, 2)),
            pltpu.SemaphoreType.REGULAR((NY // 2 + NZ // 2 - 1,)),
            dma((4, 3)),
            dma((4, 3)),
            dma((6, 3)),
            dma((6, 3)),
            dma,
            dma,
            dma,
            dma,
        ],
        compiler_params=pltpu.CompilerParams(
            collective_id=0, has_side_effects=True, vmem_limit_bytes=48 * 1024 * 1024
        ),
        name="moe_step",
    )(
        bucket_ids,
        bucket_counts,
        tokens,
        cotangent,
        expert_ids,
        gate_quant,
        gate_weight,
        up_weight,
        down_weight,
    )


def solution(mesh):
    placed = (
        P(("dp", "ep"), None),
        P(("dp", "ep"), None),
        P(("dp", "ep"), None),
        P(("dp", "ep")),
        P(),
        P("ep", "dp", None),
        P("ep", "dp", None),
        P("ep", "dp", None),
        P(("dp", "ep"), None),
    )
    return jax.shard_map(
        per_device,
        mesh=mesh,
        in_specs=placed,
        out_specs=(
            P(("dp", "ep"), None),
            P(("dp", "ep"), None),
            P("ep", "dp", None),
            P("ep", "dp", None),
            P("ep", "dp", None),
        ),
        check_vma=False,
    )
```

time: 130 us -> 75.7 us (0.58)
  Pallas kernels: 0 us -> 64.3 us
  waiting for transfers between devices: 38.3 us -> 0 us
  starting transfers between devices: 31.2 us -> 0 us
  blocking collectives: 16.6 us -> 0 us
  between operations: 14 us -> 0.66 us
  other arithmetic: 11.2 us -> 0 us
  matrix products: 6.35 us -> 0 us
  local copies, waits for them, and re-layouts: 12.2 us -> 10.3 us
    pallas_call x0 -> x1, Pallas kernels: none -> 64.3 us  [per_device(): pl.pallas_call(kernel, out_shape=[jax.ShapeDtypeStruct(tokens.shape, BF),...]
    all_to_all x2 -> x0, starting transfers between devices: 31 us -> none  [side_by_side(): lax.all_to_all(both, axis, split_axis=split_dim, concat_axis=concat_dim,...]
    all_to_all x2 -> x0, waiting for transfers between devices: 22.2 us -> none  [side_by_side(): lax.all_to_all(both, axis, split_axis=split_dim, concat_axis=concat_dim,...]
    all_gather x1 -> x0, blocking collectives: 16.6 us -> none  [per_device(): lax.all_gather(down_weight, 'dp', axis=1, tiled=True)]
    reduce_scatter x2 -> x0, waiting for transfers between devices: 16 us -> none  [the longest x1 16 us: sent_together_2(): lax.psum_scatter(both, axis, scatter_dimension=dim, tiled=True)]
    unnamed x11 -> x23, local copies, waits for them, and re-layouts: 1.35 us -> 10.3 us
    dot_general x9 -> x0, matrix products: 6.35 us -> none  [the longest x3 2.05 us: contract_rows(): lax.dot_general(left_rows, right_rows, (((0,), (0,)), ((), ())), preferre...]
    convert_element_type x5 -> x0, other arithmetic: 4.5 us -> none  [the longest x1 1.95 us: per_device(): part.astype(jnp.float32)]
  transfers between devices with their start and end apart: 5 -> 0, of which waited for: 3 -> 0; matrix products, arithmetic and copies ran while one was open for 16% -> 0% of each run, Pallas kernels for 0% -> 0%
where the time goes in v1:
time: 75.7 us; the launch traced here: 75.3 us
  Pallas kernels  64.3 us (85%)
  local copies, waits for them, and re-layouts  10.3 us (14%)
    pallas_call x1, Pallas kernels, per_device(): pl.pallas_call(kernel, out_shape=[jax.ShapeDtypeStruct(tokens.shape, BF),...  64.3 us
    unnamed x23, local copies, waits for them, and re-layouts  10.3 us

profile of v1, /device:TPU:1, one launch (start us, length us, event | category | flops | bytes accessed | tf_op | source)
XLA Modules:
  0.0 75.3 jit_solution(453071550044009271)
XLA Ops:
  0.6 0.0 copy-start
  0.6 0.9 %copy-done = bf16[1,256,384]{2,1,0:T(8,128)(2,1)S(1)} copy-done((bf16[1,256,384]{2,1,0:T(8,128)(2,1)S(1)}, bf16[1,256,384]{2,1,0:T(8,128)(2,1)}, u32[]{:S(2)}) %copy-start) | copy-done | bytes 196632
  1.6 0.0 copy-start.1
  1.6 0.9 %copy-done.1 = bf16[1,256,384]{2,1,0:T(8,128)(2,1)S(1)} copy-done((bf16[1,256,384]{2,1,0:T(8,128)(2,1)S(1)}, bf16[1,256,384]{2,1,0:T(8,128)(2,1)}, u32[]{:S(2)}) %copy-start.1) | copy-done | bytes 196632
  2.5 0.0 copy-start.2
  2.5 0.9 %copy-done.2 = bf16[1,96,1024]{2,1,0:T(8,128)(2,1)S(1)} copy-done((bf16[1,96,1024]{2,1,0:T(8,128)(2,1)S(1)}, bf16[1,96,1024]{2,1,0:T(8,128)(2,1)}, u32[]{:S(2)}) %copy-start.2) | copy-done | bytes 196632
  3.4 0.0 copy-start.3
  3.4 0.7 copy-done.3
  4.1 0.0 copy-start.4
  4.1 0.7 copy-done.4
  4.9 0.0 copy-start.5
  4.9 0.7 copy-done.5
  5.5 0.0 copy-start.6
  5.5 0.7 copy-done.6
  6.2 0.0 copy-start.7
  6.2 0.7 copy-done.7
  6.9 0.0 copy-start.8
  6.9 0.7 copy-done.8
  7.5 64.3 %moe_step.1 = (bf16[8,1024]{1,0:T(8,128)(2,1)S(1)}, bf16[8,1024]{1,0:T(8,128)(2,1)S(1)}, f32[1,256,384]{2,1,0:T(8,128)S(1)}, f32[1,256,384]{2,1,0:T(8,128)S(1)}, f32[1,96,1024]{2,1,0:T(8,128)S(1)}) custom-call(s32[8]{0:T(128)S(1)} %copy-done.7, s32[16]{0:T(128)S(1)} %copy-done.8, bf16[8,1024]{1,0:T(8,128)(2,1)S(1)} %copy-done.3, ...), custom_call_target="tpu_custom_call" | custom-call | tf_op jit(solution)/shard_map/moe_step/pallas_call | solution.py:318
  71.9 0.6 copy.19
  72.5 0.6 copy.20
  73.1 0.7 copy.21
  73.8 0.7 copy.22
  74.6 0.7 copy.23
Async XLA Ops:
  0.6 0.9 %copy-start = (bf16[1,256,384]{2,1,0:T(8,128)(2,1)S(1)}, bf16[1,256,384]{2,1,0:T(8,128)(2,1)}, u32[]{:S(2)}) copy-start(bf16[1,256,384]{2,1,0:T(8,128)(2,1)} %gate_own.1) | copy-start | bytes 589828
  1.6 0.9 %copy-start.1 = (bf16[1,256,384]{2,1,0:T(8,128)(2,1)S(1)}, bf16[1,256,384]{2,1,0:T(8,128)(2,1)}, u32[]{:S(2)}) copy-start(bf16[1,256,384]{2,1,0:T(8,128)(2,1)} %up_own.1) | copy-start | bytes 589828
  2.5 0.9 %copy-start.2 = (bf16[1,96,1024]{2,1,0:T(8,128)(2,1)S(1)}, bf16[1,96,1024]{2,1,0:T(8,128)(2,1)}, u32[]{:S(2)}) copy-start(bf16[1,96,1024]{2,1,0:T(8,128)(2,1)} %down_own.1) | copy-start | bytes 589828
  3.4 0.7 copy-start.3
  4.1 0.7 copy-start.4
  4.9 0.7 copy-start.5
  5.5 0.7 copy-start.6
  6.2 0.7 copy-start.7
  6.9 0.7 copy-start.8

commit v2 on v1

--- a/solution.py
+++ b/solution.py
@@ -11,6 +11,8 @@
 NX, NY, NZ, NC = 4, 8, 8, 2
 NE = NY * NZ * NC
 LANES = 128
+NW = 3
+GRANT = 67043328
 
 
 def dot(a, b, ca=1, cb=0):
@@ -22,20 +24,26 @@
 
 
 def kernel(
+    ids_hbm,
+    counts_hbm,
+    tokens_hbm,
+    cotangent_hbm,
+    experts_hbm,
+    quant_hbm,
+    gate_own,
+    up_own,
+    down_own,
+    layer_hbm,
+    token_hbm,
+    gate_hbm,
+    up_hbm,
+    down_hbm,
     bucket_ids,
     bucket_counts,
     tokens,
     cotangent,
     expert_ids,
     gate_quant,
-    gate_own,
-    up_own,
-    down_own,
-    layer_out,
-    token_grad,
-    gate_grad,
-    up_grad,
-    down_grad,
     gate_full,
     up_full,
     down_full,
@@ -58,7 +66,14 @@
     fin_gate,
     fin_up,
     fin_down,
-    step_sem,
+    layer_out,
+    token_grad,
+    gate_grad,
+    up_grad,
+    down_grad,
+    in_sem,
+    out_sem,
+    line_sem,
     ag_send,
     ag_recv,
     rs_send,
@@ -71,8 +86,8 @@
     x = lax.axis_index("dp")
     e = lax.axis_index("ep")
     y, z, c = e // (NZ * NC), (e // NC) % NZ, e % NC
-    tok_rows, top = expert_ids.shape
-    width = tokens.shape[1]
+    tok_rows, top = experts_hbm.shape
+    width = tokens_hbm.shape[1]
     blocks = width // LANES
     slot = 2 * blocks
 
@@ -80,16 +95,60 @@
         return (lax.rem(yy + NY, NY) * NZ + lax.rem(zz + NZ, NZ)) * NC + lax.rem(cc, NC)
 
     right, left, across = lax.rem(x + 1, NX), lax.rem(x + NX - 1, NX), lax.rem(x + 2, NX)
-    y_near = [ep(y + d, z, c) for d in (1, -1)]
-    z_near = [ep(y, z + d, c + k) for d in (1, -1) for k in (0, 1)]
-    mate = ep(y, z, c + 1)
+    column = [ep(y + d, z, c) for d in range(1, NY)]
+    shifts = [(0, 1)]
+    for d in range(1, NZ // 2 + 1):
+        shifts += [(dz, dc) for dz in sorted({d, NZ - d}) for dc in range(NC)]
+
+    shards = ((gate_own, gate_full), (up_own, up_full), (down_own, down_full))
 
     barrier = pltpu.get_barrier_semaphore()
     for xx in (right, left):
         pl.semaphore_signal(barrier, inc=1, device_id=(xx, e), device_id_type=MESH)
-    for d in (*y_near, *z_near, mate):
+    for d in (*column, *[ep(y, z + dz, c + dc) for dz, dc in shifts]):
         pl.semaphore_signal(barrier, inc=1, device_id=(x, d), device_id_type=MESH)
 
+    loads = []
+    for i, (own, full) in enumerate(shards):
+        size = own.shape[1]
+        loads.append(pltpu.make_async_copy(own.at[0], rows(full, x * size, size), in_sem.at[i]))
+    small = (
+        (experts_hbm, expert_ids),
+        (quant_hbm, gate_quant),
+        (ids_hbm, bucket_ids),
+        (counts_hbm, bucket_counts),
+        (tokens_hbm, tokens),
+        (cotangent_hbm, cotangent),
+    )
+    for i, (src, dst) in enumerate(small):
+        loads.append(pltpu.make_async_copy(src, dst, in_sem.at[NW + i]))
+    for load in loads:
+        load.start()
+    for load in loads[:NW]:
+        load.wait()
+    pl.semaphore_wait(barrier, 2 + len(column) + len(shifts))
+
+    def ag_copy(src, dst, kind, i, xx):
+        return pltpu.make_async_remote_copy(
+            src, dst, ag_send.at[kind, i], ag_recv.at[kind, i], device_id=(xx, e), device_id_type=MESH
+        )
+
+    own_right, own_left = [], []
+    for i, (own, full) in enumerate(shards):
+        size = own.shape[1]
+        part = rows(full, x * size, size)
+        own_right.append(ag_copy(part, part, 0, i, right))
+        own_left.append(ag_copy(part, part, 1, i, left))
+        own_right[i].start()
+        own_left[i].start()
+
+    for dz, dc in shifts:
+        pl.semaphore_signal(
+            line_sem.at[dz, dc], inc=1, device_id=(x, ep(y, z + dz, c + dc)), device_id_type=MESH
+        )
+
+    for load in loads[NW:]:
+        load.wait()
     lane = lax.broadcasted_iota(jnp.int32, (tok_rows, NE), 1)
     hit = jnp.zeros((tok_rows, NE), F32)
     share = jnp.zeros((tok_rows, NE), F32)
@@ -98,53 +157,29 @@
         hit = hit + jnp.where(here, 1.0, 0.0)
         share = share + jnp.where(here, gate_quant[:, k : k + 1].astype(F32), 0.0)
     share = share / 1024.0
+    pick = hit.astype(BF)
+    picked = dot(pick, tokens[...], 0, 0)
+    for j in range(blocks):
+        spread[pl.ds(j, NE, stride=slot), :] = picked[:, j * LANES : (j + 1) * LANES]
+
     row = lax.broadcasted_iota(jnp.int32, (tok_rows, NE), 0)
     count = jnp.zeros((tok_rows, NE), jnp.int32)
     for t in range(tok_rows):
         count = jnp.where(row == t, bucket_counts[bucket_ids[t]], count)
     scale = share * (64.0 / (64.0 + count.astype(F32)))
     scale_col = jnp.sum(jnp.transpose(scale), axis=1, keepdims=True)
-    pick = hit.astype(BF)
-    picked = dot(pick, tokens[...], 0, 0)
-    for j in range(blocks):
-        spread[pl.ds(j, NE, stride=slot), :] = picked[:, j * LANES : (j + 1) * LANES]
     picked = dot(pick, cotangent[...], 0, 0) * scale_col
     for j in range(blocks):
         spread[pl.ds(blocks + j, NE, stride=slot), :] = picked[:, j * LANES : (j + 1) * LANES]
+
     send[...] = spread[...].astype(BF)
 
-    pl.semaphore_wait(barrier, 9)
-
-    shards = ((gate_own, gate_full), (up_own, up_full), (down_own, down_full))
-
-    def ag_copy(src, dst, kind, i, xx):
-        return pltpu.make_async_remote_copy(
-            src, dst, ag_send.at[kind, i], ag_recv.at[kind, i], device_id=(xx, e), device_id_type=MESH
-        )
-
-    own_right, own_left = [], []
-    for i, (own, full) in enumerate(shards):
-        size = own.shape[1]
-        target = rows(full, x * size, size)
-        own_right.append(ag_copy(own.at[0], target, 0, i, right))
-        own_left.append(ag_copy(own.at[0], target, 1, i, left))
-        own_right[i].start()
-        own_left[i].start()
-
-    for s in range(NY // 2 - 1):
-        for d in y_near:
-            pl.semaphore_signal(step_sem.at[s], inc=1, device_id=(x, d), device_id_type=MESH)
-        pl.semaphore_wait(step_sem.at[s], 2)
-    for s in range(NZ // 2):
-        n = NY // 2 - 1 + s
-        peers = (*z_near, mate) if s == 0 else z_near
-        for d in peers:
-            pl.semaphore_signal(step_sem.at[n], inc=1, device_id=(x, d), device_id_type=MESH)
-        pl.semaphore_wait(step_sem.at[n], len(peers))
-
-    def exchange(src, dst, s_sem, r_sem):
-        def one(i, carry):
-            d = ep(y + i % NY, z + (i // NY) % NZ, c + i // (NY * NZ))
+    def exchange(src, dst, s_sem, r_sem, dz, dc):
+        base = ep(y, z + dz, c + dc) - y * (NZ * NC)
+        for dy in range(NY):
+            if dy + dz + dc == 0:
+                continue
+            d = lax.rem(y + dy, NY) * (NZ * NC) + base
             pltpu.make_async_remote_copy(
                 rows(src, d * slot, slot),
                 rows(dst, e * slot, slot),
@@ -153,9 +188,8 @@
                 device_id=(x, d),
                 device_id_type=MESH,
             ).start()
-            return carry
-
-        lax.fori_loop(1, NE, one, 0)
+
+    def keep(src, dst):
         at = pl.multiple_of(e * slot, slot)
         dst[pl.ds(at, slot), :] = src[pl.ds(at, slot), :]
 
@@ -163,13 +197,16 @@
         part = ref.at[pl.ds(0, (NE - 1) * slot)]
         pltpu.make_async_copy(part, part, sem).wait()
 
-    exchange(send, recv, out_send, out_recv)
+    exchange(send, recv, out_send, out_recv, 0, 0)
+    for dz, dc in shifts:
+        pl.semaphore_wait(line_sem.at[(NZ - dz) % NZ, dc], 1)
+        exchange(send, recv, out_send, out_recv, dz, dc)
+    keep(send, recv)
 
     forwards = []
     for i, (own, full) in enumerate(shards):
         size = own.shape[1]
         half = size // 2
-        full[pl.ds(pl.multiple_of(x * size, 16), size), :] = own[0]
         own_right[i].wait_recv()
         part = rows(full, left * size, half)
         forwards.append(ag_copy(part, part, 2, i, right))
@@ -245,11 +282,19 @@
     for j in range(blocks):
         spread[pl.ds(blocks + j, NE, stride=slot), :] = slot_grad[:, j * LANES : (j + 1) * LANES]
     back_send[...] = spread[...].astype(BF)
-    exchange(back_send, back_recv, ret_send, ret_recv)
+    for dz, dc in ((0, 0), *shifts):
+        exchange(back_send, back_recv, ret_send, ret_recv, dz, dc)
+    keep(back_send, back_recv)
 
     pass_on(2, part_down, hop_down, fwd_down, fin_down, down_copies)
     pass_on(0, part_gate, hop_gate, fwd_gate, fin_gate, gate_copies)
     pass_on(1, part_up, hop_up, fwd_up, fin_up, up_copies)
+
+    stores = []
+
+    def store(src, dst):
+        stores.append(pltpu.make_async_copy(src, dst, out_sem.at[len(stores)]))
+        stores[-1].start()
 
     def finish(part, fin, out, copies):
         size = part.shape[0] // NX
@@ -263,6 +308,7 @@
             )
 
     finish(part_down, fin_down, down_grad, down_copies)
+    store(down_grad, down_hbm)
 
     wait_all(back_recv, ret_recv)
     spread[...] = back_recv[...].astype(F32)
@@ -275,13 +321,33 @@
         grads = spread[pl.ds(blocks + j, NE, stride=slot), :].astype(BF)
         token_grad[:, at] = dot(pick, grads).astype(BF)
 
+    store(layer_out, layer_hbm)
+    store(token_grad, token_hbm)
     finish(part_gate, fin_gate, gate_grad, gate_copies)
+    store(gate_grad, gate_hbm)
     finish(part_up, fin_up, up_grad, up_copies)
+    store(up_grad, up_hbm)
 
     for k in (*own_right, *own_left, *forwards, *down_copies, *gate_copies, *up_copies):
         k.wait_send()
     wait_all(send, out_send)
     wait_all(back_send, ret_send)
+    for k in stores:
+        k.wait()
+
+
+def emit(*refs):
+    n = len(refs) // 3
+    arrays, outs, held, sem = refs[:n], refs[n : 2 * n], refs[2 * n : 3 * n], refs[3 * n]
+    reads = [pltpu.make_async_copy(arrays[i], held[i], sem.at[i]) for i in range(n)]
+    writes = [pltpu.make_async_copy(held[i], outs[i], sem.at[n + i]) for i in range(n)]
+    for k in reads:
+        k.start()
+    for i in range(n):
+        reads[i].wait()
+        writes[i].start()
+    for k in writes:
+        k.wait()
 
 
 def per_device(
@@ -298,8 +364,7 @@
     width = tokens.shape[1]
     _, share, hidden = gate_weight.shape
     deep = down_weight.shape[1]
-    vmem = pl.BlockSpec(memory_space=pltpu.VMEM)
-    smem = pl.BlockSpec(memory_space=pltpu.SMEM)
+    hbm = pl.BlockSpec(memory_space=pltpu.HBM)
     slots = (NE * 2 * (width // LANES), LANES)
 
     def pieces(lead):
@@ -315,7 +380,7 @@
         pltpu.VMEM((hidden, width), BF),
     ]
     dma = pltpu.SemaphoreType.DMA
-    return pl.pallas_call(
+    results = pl.pallas_call(
         kernel,
         out_shape=[
             jax.ShapeDtypeStruct(tokens.shape, BF),
@@ -324,9 +389,15 @@
             jax.ShapeDtypeStruct(up_weight.shape, F32),
             jax.ShapeDtypeStruct(down_weight.shape, F32),
         ],
-        in_specs=[smem] * 2 + [vmem] * 7,
-        out_specs=[vmem] * 5,
+        in_specs=[hbm] * 9,
+        out_specs=[hbm] * 5,
         scratch_shapes=[
+            pltpu.SMEM(bucket_ids.shape, jnp.int32),
+            pltpu.SMEM(bucket_counts.shape, jnp.int32),
+            pltpu.VMEM(tokens.shape, BF),
+            pltpu.VMEM(tokens.shape, BF),
+            pltpu.VMEM(expert_ids.shape, jnp.int32),
+            pltpu.VMEM(expert_ids.shape, jnp.int32),
             *full,
             *[pltpu.VMEM(slots, BF)] * 4,
             pltpu.VMEM(slots, F32),
@@ -335,7 +406,14 @@
             *pieces((2,)),
             *pieces((2,)),
             *pieces((2, 2)),
-            pltpu.SemaphoreType.REGULAR((NY // 2 + NZ // 2 - 1,)),
+            pltpu.VMEM(tokens.shape, BF),
+            pltpu.VMEM(tokens.shape, BF),
+            pltpu.VMEM(gate_weight.shape, F32),
+            pltpu.VMEM(up_weight.shape, F32),
+            pltpu.VMEM(down_weight.shape, F32),
+            dma((NW + 6,)),
+            dma((5,)),
+            pltpu.SemaphoreType.REGULAR((NZ, NC)),
             dma((4, 3)),
             dma((4, 3)),
             dma((6, 3)),
@@ -346,7 +424,7 @@
             dma,
         ],
         compiler_params=pltpu.CompilerParams(
-            collective_id=0, has_side_effects=True, vmem_limit_bytes=48 * 1024 * 1024
+            collective_id=0, has_side_effects=True, vmem_limit_bytes=GRANT
         ),
         name="moe_step",
     )(
@@ -360,6 +438,15 @@
         up_weight,
         down_weight,
     )
+    return pl.pallas_call(
+        emit,
+        out_shape=[jax.ShapeDtypeStruct(r.shape, r.dtype) for r in results],
+        in_specs=[hbm] * len(results),
+        out_specs=[hbm] * len(results),
+        scratch_shapes=[*[pltpu.VMEM(r.shape, r.dtype) for r in results], dma((2 * len(results),))],
+        compiler_params=pltpu.CompilerParams(vmem_limit_bytes=GRANT),
+        name="emit",
+    )(*results)
 
 
 def solution(mesh):

time: 75.7 us -> 60.9 us (0.80)
  local copies, waits for them, and re-layouts: 10.3 us -> 0 us
  Pallas kernels: 64.3 us -> 60 us
    unnamed x23 -> x0, local copies, waits for them, and re-layouts: 10.3 us -> none
    pallas_call x1, Pallas kernels: 64.3 us -> 57.9 us  [per_device(): pl.pallas_call(kernel, out_shape=[jax.ShapeDtypeStruct(tokens.shape, BF),...]
    pallas_call x0 -> x1, Pallas kernels: none -> 2.12 us  [per_device(): pl.pallas_call(emit, out_shape=[jax.ShapeDtypeStruct(r.shape, r.dtype) fo...]
where the time goes in v2:
time: 60.9 us; the launch traced here: 60.7 us
  Pallas kernels  60 us (99%)
  between operations  0.64 us (1%)
    pallas_call x1, Pallas kernels, per_device(): pl.pallas_call(kernel, out_shape=[jax.ShapeDtypeStruct(tokens.shape, BF),...  57.9 us
    pallas_call x1, Pallas kernels, per_device(): pl.pallas_call(emit, out_shape=[jax.ShapeDtypeStruct(r.shape, r.dtype) fo...  2.12 us

profile of v2, /device:TPU:1, one launch (start us, length us, event | category | flops | bytes accessed | tf_op | source)
XLA Modules:
  0.0 60.7 jit_solution(10642453055366130692)
XLA Ops:
  0.6 57.9 %moe_step.1 = (bf16[8,1024]{1,0:T(8,128)(2,1)}, bf16[8,1024]{1,0:T(8,128)(2,1)}, f32[1,256,384]{2,1,0:T(8,128)}, f32[1,256,384]{2,1,0:T(8,128)}, f32[1,96,1024]{2,1,0:T(8,128)}) custom-call(s32[8]{0:T(128)} %ids_hbm.1, s32[16]{0:T(128)} %counts_hbm.1, bf16[8,1024]{1,0:T(8,128)(2,1)} %tokens_hbm.1, bf16[8,1024]{1,0:T(8,128)(2,1)} %cotangent_hbm.1, ...), custom_call_target="tpu_custom_call" | custom-call | tf_op jit(solution)/shard_map/moe_step/pallas_call | solution.py:383
  58.5 2.1 %emit.1 = (bf16[8,1024]{1,0:T(8,128)(2,1)}, bf16[8,1024]{1,0:T(8,128)(2,1)}, f32[1,256,384]{2,1,0:T(8,128)}, f32[1,256,384]{2,1,0:T(8,128)}, f32[1,96,1024]{2,1,0:T(8,128)}) custom-call(bf16[8,1024]{1,0:T(8,128)(2,1)} %get-tuple-element.10.refs_0_, bf16[8,1024]{1,0:T(8,128)(2,1)} %get-tuple-element.11.refs_1_, f32[1,256,384]{2,1,0:T(8,128)} %get-tuple-element.12.refs_2_, ...), custom_call_target="tpu_custom_call" | custom-call | tf_op jit(solution)/shard_map/emit/pallas_call | solution.py:441

commit v3 on v2

--- a/solution.py
+++ b/solution.py
@@ -12,7 +12,7 @@
 NE = NY * NZ * NC
 LANES = 128
 NW = 3
-GRANT = 67043328
+GRANT = 67043328 - 1280 * 1024
 
 
 def dot(a, b, ca=1, cb=0):
@@ -33,11 +33,11 @@
     gate_own,
     up_own,
     down_own,
-    layer_hbm,
-    token_hbm,
-    gate_hbm,
-    up_hbm,
-    down_hbm,
+    layer_out,
+    token_grad,
+    gate_grad,
+    up_grad,
+    down_grad,
     bucket_ids,
     bucket_counts,
     tokens,
@@ -66,13 +66,7 @@
     fin_gate,
     fin_up,
     fin_down,
-    layer_out,
-    token_grad,
-    gate_grad,
-    up_grad,
-    down_grad,
     in_sem,
-    out_sem,
     line_sem,
     ag_send,
     ag_recv,
@@ -270,11 +264,6 @@
     hidden_grad = dot(scaled[...], down_full[...], 1, 1)
     gate_pre = (hidden_grad * pre_up * (sig * (1.0 + pre_gate * (1.0 - sig)))).astype(BF)
     up_pre = (hidden_grad * act).astype(BF)
-    part_gate[...] = dot(rows_in[...], gate_pre, 0, 0).astype(BF)
-    gate_copies = scatter(0, part_gate, hop_gate, fin_gate)
-    part_up[...] = dot(rows_in[...], up_pre, 0, 0).astype(BF)
-    up_copies = scatter(1, part_up, hop_up, fin_up)
-
     expert_out = dot(hidden, down_full[...])
     for j in range(blocks):
         spread[pl.ds(j, NE, stride=slot), :] = expert_out[:, j * LANES : (j + 1) * LANES]
@@ -286,15 +275,14 @@
         exchange(back_send, back_recv, ret_send, ret_recv, dz, dc)
     keep(back_send, back_recv)
 
+    part_gate[...] = dot(rows_in[...], gate_pre, 0, 0).astype(BF)
+    gate_copies = scatter(0, part_gate, hop_gate, fin_gate)
+    part_up[...] = dot(rows_in[...], up_pre, 0, 0).astype(BF)
+    up_copies = scatter(1, part_up, hop_up, fin_up)
+
     pass_on(2, part_down, hop_down, fwd_down, fin_down, down_copies)
     pass_on(0, part_gate, hop_gate, fwd_gate, fin_gate, gate_copies)
     pass_on(1, part_up, hop_up, fwd_up, fin_up, up_copies)
-
-    stores = []
-
-    def store(src, dst):
-        stores.append(pltpu.make_async_copy(src, dst, out_sem.at[len(stores)]))
-        stores[-1].start()
 
     def finish(part, fin, out, copies):
         size = part.shape[0] // NX
@@ -308,7 +296,6 @@
             )
 
     finish(part_down, fin_down, down_grad, down_copies)
-    store(down_grad, down_hbm)
 
     wait_all(back_recv, ret_recv)
     spread[...] = back_recv[...].astype(F32)
@@ -321,32 +308,22 @@
         grads = spread[pl.ds(blocks + j, NE, stride=slot), :].astype(BF)
         token_grad[:, at] = dot(pick, grads).astype(BF)
 
-    store(layer_out, layer_hbm)
-    store(token_grad, token_hbm)
     finish(part_gate, fin_gate, gate_grad, gate_copies)
-    store(gate_grad, gate_hbm)
     finish(part_up, fin_up, up_grad, up_copies)
-    store(up_grad, up_hbm)
 
     for k in (*own_right, *own_left, *forwards, *down_copies, *gate_copies, *up_copies):
         k.wait_send()
     wait_all(send, out_send)
     wait_all(back_send, ret_send)
-    for k in stores:
-        k.wait()
 
 
 def emit(*refs):
-    n = len(refs) // 3
-    arrays, outs, held, sem = refs[:n], refs[n : 2 * n], refs[2 * n : 3 * n], refs[3 * n]
-    reads = [pltpu.make_async_copy(arrays[i], held[i], sem.at[i]) for i in range(n)]
-    writes = [pltpu.make_async_copy(held[i], outs[i], sem.at[n + i]) for i in range(n)]
-    for k in reads:
+    *arrays, sem = refs
+    half = len(arrays) // 2
+    copies = [pltpu.make_async_copy(arrays[i], arrays[half + i], sem.at[i]) for i in range(half)]
+    for k in copies:
         k.start()
-    for i in range(n):
-        reads[i].wait()
-        writes[i].start()
-    for k in writes:
+    for k in copies:
         k.wait()
 
 
@@ -365,6 +342,7 @@
     _, share, hidden = gate_weight.shape
     deep = down_weight.shape[1]
     hbm = pl.BlockSpec(memory_space=pltpu.HBM)
+    vmem = pl.BlockSpec(memory_space=pltpu.VMEM)
     slots = (NE * 2 * (width // LANES), LANES)
 
     def pieces(lead):
@@ -383,14 +361,14 @@
     results = pl.pallas_call(
         kernel,
         out_shape=[
-            jax.ShapeDtypeStruct(tokens.shape, BF),
-            jax.ShapeDtypeStruct(tokens.shape, BF),
-            jax.ShapeDtypeStruct(gate_weight.shape, F32),
-            jax.ShapeDtypeStruct(up_weight.shape, F32),
-            jax.ShapeDtypeStruct(down_weight.shape, F32),
+            pltpu.VMEM(tokens.shape, BF),
+            pltpu.VMEM(tokens.shape, BF),
+            pltpu.VMEM(gate_weight.shape, F32),
+            pltpu.VMEM(up_weight.shape, F32),
+            pltpu.VMEM(down_weight.shape, F32),
         ],
         in_specs=[hbm] * 9,
-        out_specs=[hbm] * 5,
+        out_specs=[vmem] * 5,
         scratch_shapes=[
             pltpu.SMEM(bucket_ids.shape, jnp.int32),
             pltpu.SMEM(bucket_counts.shape, jnp.int32),
@@ -406,13 +384,7 @@
             *pieces((2,)),
             *pieces((2,)),
             *pieces((2, 2)),
-            pltpu.VMEM(tokens.shape, BF),
-            pltpu.VMEM(tokens.shape, BF),
-            pltpu.VMEM(gate_weight.shape, F32),
-            pltpu.VMEM(up_weight.shape, F32),
-            pltpu.VMEM(down_weight.shape, F32),
             dma((NW + 6,)),
-            dma((5,)),
             pltpu.SemaphoreType.REGULAR((NZ, NC)),
             dma((4, 3)),
             dma((4, 3)),
@@ -441,10 +413,10 @@
     return pl.pallas_call(
         emit,
         out_shape=[jax.ShapeDtypeStruct(r.shape, r.dtype) for r in results],
-        in_specs=[hbm] * len(results),
+        in_specs=[vmem] * len(results),
         out_specs=[hbm] * len(results),
-        scratch_shapes=[*[pltpu.VMEM(r.shape, r.dtype) for r in results], dma((2 * len(results),))],
-        compiler_params=pltpu.CompilerParams(vmem_limit_bytes=GRANT),
+        scratch_shapes=[dma((len(results),))],
+        compiler_params=pltpu.CompilerParams(vmem_limit_bytes=32 * 1024 * 1024),
         name="emit",
     )(*results)
 

time: 60.9 us -> 58.3 us (0.957)
  Pallas kernels: 60 us -> 57.5 us
    pallas_call x1, Pallas kernels: 57.9 us -> 56.5 us  [per_device(): pl.pallas_call(kernel, out_shape=[pltpu.VMEM(tokens.shape, BF), pltpu.VME...]
    pallas_call x1, Pallas kernels: 2.12 us -> 1.06 us  [per_device(): pl.pallas_call(emit, out_shape=[jax.ShapeDtypeStruct(r.shape, r.dtype) fo...]
where the time goes in v3:
time: 58.3 us; the launch traced here: 58.2 us
  Pallas kernels  57.5 us (99%)
  between operations  0.64 us (1%)
    pallas_call x1, Pallas kernels, per_device(): pl.pallas_call(kernel, out_shape=[pltpu.VMEM(tokens.shape, BF), pltpu.VME...  56.5 us

profile of v3, /device:TPU:1, one launch (start us, length us, event | category | flops | bytes accessed | tf_op | source)
XLA Modules:
  0.0 58.2 jit_solution(6778467864604888328)
XLA Ops:
  0.6 56.5 %moe_step.1 = (bf16[8,1024]{1,0:T(8,128)(2,1)S(1)}, bf16[8,1024]{1,0:T(8,128)(2,1)S(1)}, f32[1,256,384]{2,1,0:T(8,128)S(1)}, f32[1,256,384]{2,1,0:T(8,128)S(1)}, f32[1,96,1024]{2,1,0:T(8,128)S(1)}) custom-call(s32[8]{0:T(128)} %ids_hbm.1, s32[16]{0:T(128)} %counts_hbm.1, bf16[8,1024]{1,0:T(8,128)(2,1)} %tokens_hbm.1, bf16[8,1024]{1,0:T(8,128)(2,1)} %cotangent_hbm.1, ...), custom_call_target="tpu_custom_call" | custom-call | tf_op jit(solution)/shard_map/moe_step/pallas_call | solution.py:361
  57.1 1.1 %emit.1 = (bf16[8,1024]{1,0:T(8,128)(2,1)}, bf16[8,1024]{1,0:T(8,128)(2,1)}, f32[1,256,384]{2,1,0:T(8,128)}, f32[1,256,384]{2,1,0:T(8,128)}, f32[1,96,1024]{2,1,0:T(8,128)}) custom-call(bf16[8,1024]{1,0:T(8,128)(2,1)S(1)} %get-tuple-element.10.refs_0_, bf16[8,1024]{1,0:T(8,128)(2,1)S(1)} %get-tuple-element.11.refs_1_, ...), custom_call_target="tpu_custom_call" | custom-call | tf_op jit(solution)/shard_map/emit/pallas_call | solution.py:413

commit v4 on v3

--- a/solution.py
+++ b/solution.py
@@ -54,22 +54,20 @@
     spread,
     rows_in,
     scaled,
-    part_gate,
-    part_up,
+    tok_all,
+    pre_all,
     part_down,
-    hop_gate,
-    hop_up,
     hop_down,
-    fwd_gate,
-    fwd_up,
     fwd_down,
-    fin_gate,
-    fin_up,
     fin_down,
     in_sem,
     line_sem,
     ag_send,
     ag_recv,
+    tok_send,
+    tok_recv,
+    pre_send,
+    pre_recv,
     rs_send,
     rs_recv,
     out_send,
@@ -118,8 +116,6 @@
         loads.append(pltpu.make_async_copy(src, dst, in_sem.at[NW + i]))
     for load in loads:
         load.start()
-    for load in loads[:NW]:
-        load.wait()
     pl.semaphore_wait(barrier, 2 + len(column) + len(shifts))
 
     def ag_copy(src, dst, kind, i, xx):
@@ -131,8 +127,8 @@
     for i, (own, full) in enumerate(shards):
         size = own.shape[1]
         part = rows(full, x * size, size)
-        own_right.append(ag_copy(part, part, 0, i, right))
-        own_left.append(ag_copy(part, part, 1, i, left))
+        own_right.append(ag_copy(own.at[0], part, 0, i, right))
+        own_left.append(ag_copy(own.at[0], part, 1, i, left))
         own_right[i].start()
         own_left[i].start()
 
@@ -141,7 +137,7 @@
             line_sem.at[dz, dc], inc=1, device_id=(x, ep(y, z + dz, c + dc)), device_id_type=MESH
         )
 
-    for load in loads[NW:]:
+    for load in loads:
         load.wait()
     lane = lax.broadcasted_iota(jnp.int32, (tok_rows, NE), 1)
     hit = jnp.zeros((tok_rows, NE), F32)
@@ -168,12 +164,12 @@
 
     send[...] = spread[...].astype(BF)
 
-    def exchange(src, dst, s_sem, r_sem, dz, dc):
-        base = ep(y, z + dz, c + dc) - y * (NZ * NC)
-        for dy in range(NY):
-            if dy + dz + dc == 0:
-                continue
-            d = lax.rem(y + dy, NY) * (NZ * NC) + base
+    def hops(dy, dz):
+        return min(dy, NY - dy) + min(dz, NZ - dz)
+
+    def exchange(src, dst, s_sem, r_sem, where):
+        for dy, dz, dc in where:
+            d = ep(y + dy, z + dz, c + dc)
             pltpu.make_async_remote_copy(
                 rows(src, d * slot, slot),
                 rows(dst, e * slot, slot),
@@ -183,6 +179,10 @@
                 device_id_type=MESH,
             ).start()
 
+    def line(dz, dc):
+        there = [(dy, dz, dc) for dy in range(NY) if dy + dz + dc]
+        return sorted(there, key=lambda k: -hops(k[0], k[1]))
+
     def keep(src, dst):
         at = pl.multiple_of(e * slot, slot)
         dst[pl.ds(at, slot), :] = src[pl.ds(at, slot), :]
@@ -191,10 +191,10 @@
         part = ref.at[pl.ds(0, (NE - 1) * slot)]
         pltpu.make_async_copy(part, part, sem).wait()
 
-    exchange(send, recv, out_send, out_recv, 0, 0)
+    exchange(send, recv, out_send, out_recv, line(0, 0))
     for dz, dc in shifts:
         pl.semaphore_wait(line_sem.at[(NZ - dz) % NZ, dc], 1)
-        exchange(send, recv, out_send, out_recv, dz, dc)
+        exchange(send, recv, out_send, out_recv, line(dz, dc))
     keep(send, recv)
 
     forwards = []
@@ -212,58 +212,91 @@
 
     wait_all(recv, out_recv)
     spread[...] = recv[...].astype(F32)
-    for j in range(blocks):
-        at = slice(j * LANES, (j + 1) * LANES)
-        rows_in[:, at] = spread[pl.ds(j, NE, stride=slot), :].astype(BF)
-        scaled[:, at] = spread[pl.ds(blocks + j, NE, stride=slot), :].astype(BF)
+    per = blocks // NX
+    for j in range(blocks):
+        at = slice(j % per * LANES, (j % per + 1) * LANES)
+        rows_in[j // per, :, at] = spread[pl.ds(j, NE, stride=slot), :].astype(BF)
+
+    tok_copies = []
+    for i, xx in enumerate((right, left, across)):
+        tok_copies.append(
+            pltpu.make_async_remote_copy(
+                rows_in.at[xx],
+                tok_all.at[x],
+                tok_send.at[i],
+                tok_recv.at[i],
+                device_id=(xx, e),
+                device_id_type=MESH,
+            )
+        )
+        tok_copies[-1].start()
+    for j in range(blocks):
+        scaled[:, j * LANES : (j + 1) * LANES] = spread[pl.ds(blocks + j, NE, stride=slot), :].astype(BF)
     for f in forwards[:4]:
         f.wait_recv()
-    pre_gate = dot(rows_in[...], gate_full[...])
-    pre_up = dot(rows_in[...], up_full[...])
+    deep = gate_own.shape[1]
+    pre_gate = jnp.zeros((NE, gate_full.shape[1]), F32)
+    pre_up = jnp.zeros((NE, gate_full.shape[1]), F32)
+    for q in range(NX):
+        at = slice(q * deep, (q + 1) * deep)
+        pre_gate = pre_gate + dot(rows_in[q], gate_full[at, :])
+        pre_up = pre_up + dot(rows_in[q], up_full[at, :])
     sig = jax.nn.sigmoid(pre_gate)
     act = pre_gate * sig
     hidden = (act * pre_up).astype(BF)
 
-    def rs_copy(src, dst, kind, i, xx):
+    def rs_copy(src, dst, kind, xx):
         return pltpu.make_async_remote_copy(
-            src, dst, rs_send.at[kind, i], rs_recv.at[kind, i], device_id=(xx, e), device_id_type=MESH
+            src, dst, rs_send.at[kind], rs_recv.at[kind], device_id=(xx, e), device_id_type=MESH
         )
 
-    def scatter(i, part, hop, fin):
+    def scatter(part, hop, fin):
         size = part.shape[0] // NX
         half = size // 2
         copies = [
-            rs_copy(rows(part, across * size, half), hop.at[0], 0, i, right),
-            rs_copy(rows(part, across * size + half, half), hop.at[1], 1, i, left),
-            rs_copy(rows(part, right * size + half, half), fin.at[0, 1], 2, i, right),
-            rs_copy(rows(part, left * size, half), fin.at[1, 0], 3, i, left),
+            rs_copy(rows(part, across * size, half), hop.at[0], 0, right),
+            rs_copy(rows(part, across * size + half, half), hop.at[1], 1, left),
+            rs_copy(rows(part, right * size + half, half), fin.at[0, 1], 2, right),
+            rs_copy(rows(part, left * size, half), fin.at[1, 0], 3, left),
         ]
         for k in copies:
             k.start()
         return copies
 
-    def pass_on(i, part, hop, fwd, fin, copies):
+    def pass_on(part, hop, fwd, fin, copies):
         size = part.shape[0] // NX
         half = size // 2
         copies[0].wait_recv()
         mine = part[pl.ds(pl.multiple_of(right * size, 16), half), :]
         fwd[0] = (hop[0].astype(F32) + mine.astype(F32)).astype(BF)
-        copies.append(rs_copy(fwd.at[0], fin.at[0, 0], 4, i, right))
+        copies.append(rs_copy(fwd.at[0], fin.at[0, 0], 4, right))
         copies[-1].start()
         copies[1].wait_recv()
         mine = part[pl.ds(pl.multiple_of(left * size + half, 16), half), :]
         fwd[1] = (hop[1].astype(F32) + mine.astype(F32)).astype(BF)
-        copies.append(rs_copy(fwd.at[1], fin.at[1, 1], 5, i, left))
+        copies.append(rs_copy(fwd.at[1], fin.at[1, 1], 5, left))
         copies[-1].start()
 
     part_down[...] = dot(hidden, scaled[...], 0, 0).astype(BF)
-    down_copies = scatter(2, part_down, hop_down, fin_down)
+    down_copies = scatter(part_down, hop_down, fin_down)
 
     for f in forwards[4:]:
         f.wait_recv()
     hidden_grad = dot(scaled[...], down_full[...], 1, 1)
     gate_pre = (hidden_grad * pre_up * (sig * (1.0 + pre_gate * (1.0 - sig)))).astype(BF)
     up_pre = (hidden_grad * act).astype(BF)
+    pre_all[x, 0] = gate_pre
+    pre_all[x, 1] = up_pre
+
+    def pre_copy(ref, kind, xx):
+        return pltpu.make_async_remote_copy(
+            ref, ref, pre_send.at[kind], pre_recv.at[kind], device_id=(xx, e), device_id_type=MESH
+        )
+
+    pre_copies = [pre_copy(pre_all.at[x], 0, right), pre_copy(pre_all.at[x], 1, left)]
+    for k in pre_copies:
+        k.start()
+
     expert_out = dot(hidden, down_full[...])
     for j in range(blocks):
         spread[pl.ds(j, NE, stride=slot), :] = expert_out[:, j * LANES : (j + 1) * LANES]
@@ -271,18 +304,15 @@
     for j in range(blocks):
         spread[pl.ds(blocks + j, NE, stride=slot), :] = slot_grad[:, j * LANES : (j + 1) * LANES]
     back_send[...] = spread[...].astype(BF)
-    for dz, dc in ((0, 0), *shifts):
-        exchange(back_send, back_recv, ret_send, ret_recv, dz, dc)
+    everyone = [k for dz, dc in ((0, 0), *shifts) for k in line(dz, dc)]
+    exchange(back_send, back_recv, ret_send, ret_recv, sorted(everyone, key=lambda k: -hops(k[0], k[1])))
     keep(back_send, back_recv)
 
-    part_gate[...] = dot(rows_in[...], gate_pre, 0, 0).astype(BF)
-    gate_copies = scatter(0, part_gate, hop_gate, fin_gate)
-    part_up[...] = dot(rows_in[...], up_pre, 0, 0).astype(BF)
-    up_copies = scatter(1, part_up, hop_up, fin_up)
-
-    pass_on(2, part_down, hop_down, fwd_down, fin_down, down_copies)
-    pass_on(0, part_gate, hop_gate, fwd_gate, fin_gate, gate_copies)
-    pass_on(1, part_up, hop_up, fwd_up, fin_up, up_copies)
+    pass_on(part_down, hop_down, fwd_down, fin_down, down_copies)
+    for kind, xx, source in ((0, right, left), (1, left, right)):
+        pre_copies[kind].wait_recv()
+        pre_copies.append(pre_copy(pre_all.at[source, kind], 2 + kind, xx))
+        pre_copies[-1].start()
 
     def finish(part, fin, out, copies):
         size = part.shape[0] // NX
@@ -295,7 +325,18 @@
                 mine.astype(F32) + fin[0, h].astype(F32) + fin[1, h].astype(F32)
             )
 
+    for k in tok_copies:
+        k.wait_recv()
+    sum_gate = dot(rows_in[x], gate_pre, 0, 0)
+    sum_up = dot(rows_in[x], up_pre, 0, 0)
+    for xx in (left, right):
+        sum_gate = sum_gate + dot(tok_all[xx], pre_all[xx, 0], 0, 0)
+        sum_up = sum_up + dot(tok_all[xx], pre_all[xx, 1], 0, 0)
     finish(part_down, fin_down, down_grad, down_copies)
+    for k in pre_copies[2:]:
+        k.wait_recv()
+    gate_grad[0] = sum_gate + dot(tok_all[across], pre_all[across, 0], 0, 0)
+    up_grad[0] = sum_up + dot(tok_all[across], pre_all[across, 1], 0, 0)
 
     wait_all(back_recv, ret_recv)
     spread[...] = back_recv[...].astype(F32)
@@ -308,10 +349,7 @@
         grads = spread[pl.ds(blocks + j, NE, stride=slot), :].astype(BF)
         token_grad[:, at] = dot(pick, grads).astype(BF)
 
-    finish(part_gate, fin_gate, gate_grad, gate_copies)
-    finish(part_up, fin_up, up_grad, up_copies)
-
-    for k in (*own_right, *own_left, *forwards, *down_copies, *gate_copies, *up_copies):
+    for k in (*own_right, *own_left, *forwards, *tok_copies, *pre_copies, *down_copies):
         k.wait_send()
     wait_all(send, out_send)
     wait_all(back_send, ret_send)
@@ -344,13 +382,6 @@
     hbm = pl.BlockSpec(memory_space=pltpu.HBM)
     vmem = pl.BlockSpec(memory_space=pltpu.VMEM)
     slots = (NE * 2 * (width // LANES), LANES)
-
-    def pieces(lead):
-        return [
-            pltpu.VMEM((*lead, share // 2, hidden), BF),
-            pltpu.VMEM((*lead, share // 2, hidden), BF),
-            pltpu.VMEM((*lead, deep // 2, width), BF),
-        ]
 
     full = [
         pltpu.VMEM((width, hidden), BF),
@@ -379,17 +410,24 @@
             *full,
             *[pltpu.VMEM(slots, BF)] * 4,
             pltpu.VMEM(slots, F32),
-            *[pltpu.VMEM((NE, width), BF)] * 2,
-            *full,
-            *pieces((2,)),
-            *pieces((2,)),
-            *pieces((2, 2)),
+            pltpu.VMEM((NX, NE, share), BF),
+            pltpu.VMEM((NE, width), BF),
+            pltpu.VMEM((NX, NE, share), BF),
+            pltpu.VMEM((NX, 2, NE, hidden), BF),
+            pltpu.VMEM((hidden, width), BF),
+            pltpu.VMEM((2, deep // 2, width), BF),
+            pltpu.VMEM((2, deep // 2, width), BF),
+            pltpu.VMEM((2, 2, deep // 2, width), BF),
             dma((NW + 6,)),
             pltpu.SemaphoreType.REGULAR((NZ, NC)),
             dma((4, 3)),
             dma((4, 3)),
-            dma((6, 3)),
-            dma((6, 3)),
+            dma((3,)),
+            dma((3,)),
+            dma((4,)),
+            dma((4,)),
+            dma((6,)),
+            dma((6,)),
             dma,
             dma,
             dma,

time: 58.3 us -> 54.9 us (0.942)
  Pallas kernels: 57.5 us -> 54.1 us
    pallas_call x1, Pallas kernels: 56.5 us -> 53.1 us  [per_device(): pl.pallas_call(kernel, out_shape=[pltpu.VMEM(tokens.shape, BF), pltpu.VME...]
where the time goes in v4:
time: 54.9 us; the launch traced here: 54.8 us
  Pallas kernels  54.1 us (99%)
  between operations  0.64 us (1%)
    pallas_call x1, Pallas kernels, per_device(): pl.pallas_call(kernel, out_shape=[pltpu.VMEM(tokens.shape, BF), pltpu.VME...  53.1 us

profile of v4, /device:TPU:1, one launch (start us, length us, event | category | flops | bytes accessed | tf_op | source)
XLA Modules:
  0.0 54.8 jit_solution(6372888415365662717)
XLA Ops:
  0.6 53.1 %moe_step.1 = (bf16[8,1024]{1,0:T(8,128)(2,1)S(1)}, bf16[8,1024]{1,0:T(8,128)(2,1)S(1)}, f32[1,256,384]{2,1,0:T(8,128)S(1)}, f32[1,256,384]{2,1,0:T(8,128)S(1)}, f32[1,96,1024]{2,1,0:T(8,128)S(1)}) custom-call(s32[8]{0:T(128)} %ids_hbm.1, s32[16]{0:T(128)} %counts_hbm.1, bf16[8,1024]{1,0:T(8,128)(2,1)} %tokens_hbm.1, bf16[8,1024]{1,0:T(8,128)(2,1)} %cotangent_hbm.1, ...), custom_call_target="tpu_custom_call" | custom-call | tf_op jit(solution)/shard_map/moe_step/pallas_call | solution.py:392
  53.7 1.1 %emit.1 = (bf16[8,1024]{1,0:T(8,128)(2,1)}, bf16[8,1024]{1,0:T(8,128)(2,1)}, f32[1,256,384]{2,1,0:T(8,128)}, f32[1,256,384]{2,1,0:T(8,128)}, f32[1,96,1024]{2,1,0:T(8,128)}) custom-call(bf16[8,1024]{1,0:T(8,128)(2,1)S(1)} %get-tuple-element.10.refs_0_, bf16[8,1024]{1,0:T(8,128)(2,1)S(1)} %get-tuple-element.11.refs_1_, ...), custom_call_target="tpu_custom_call" | custom-call | tf_op jit(solution)/shard_map/emit/pallas_call | solution.py:451

commit v5 on v4

--- a/solution.py
+++ b/solution.py
@@ -49,11 +49,18 @@
     down_full,
     send,
     recv,
-    back_send,
-    back_recv,
+    outs_send,
+    outs_recv,
+    grads_send,
+    grads_recv,
     spread,
     rows_in,
     scaled,
+    tok_src,
+    ids_all,
+    more_send,
+    more_recv,
+    spread_more,
     tok_all,
     pre_all,
     part_down,
@@ -64,8 +71,11 @@
     line_sem,
     ag_send,
     ag_recv,
-    tok_send,
-    tok_recv,
+    src_send,
+    src_recv,
+    src_own,
+    ext_send,
+    ext_recv,
     pre_send,
     pre_recv,
     rs_send,
@@ -82,6 +92,7 @@
     width = tokens_hbm.shape[1]
     blocks = width // LANES
     slot = 2 * blocks
+    per = blocks // NX
 
     def ep(yy, zz, cc):
         return (lax.rem(yy + NY, NY) * NZ + lax.rem(zz + NZ, NZ)) * NC + lax.rem(cc, NC)
@@ -93,12 +104,6 @@
         shifts += [(dz, dc) for dz in sorted({d, NZ - d}) for dc in range(NC)]
 
     shards = ((gate_own, gate_full), (up_own, up_full), (down_own, down_full))
-
-    barrier = pltpu.get_barrier_semaphore()
-    for xx in (right, left):
-        pl.semaphore_signal(barrier, inc=1, device_id=(xx, e), device_id_type=MESH)
-    for d in (*column, *[ep(y, z + dz, c + dc) for dz, dc in shifts]):
-        pl.semaphore_signal(barrier, inc=1, device_id=(x, d), device_id_type=MESH)
 
     loads = []
     for i, (own, full) in enumerate(shards):
@@ -116,7 +121,16 @@
         loads.append(pltpu.make_async_copy(src, dst, in_sem.at[NW + i]))
     for load in loads:
         load.start()
-    pl.semaphore_wait(barrier, 2 + len(column) + len(shifts))
+
+    barrier = pltpu.get_barrier_semaphore()
+    for xx in (right, left, across):
+        pl.semaphore_signal(barrier, inc=1, device_id=(xx, e), device_id_type=MESH)
+    for d in (*column, *[ep(y, z + dz, c + dc) for dz, dc in shifts]):
+        pl.semaphore_signal(barrier, inc=1, device_id=(x, d), device_id_type=MESH)
+
+    for load in loads[:NW]:
+        load.wait()
+    pl.semaphore_wait(barrier, 3 + len(column) + len(shifts))
 
     def ag_copy(src, dst, kind, i, xx):
         return pltpu.make_async_remote_copy(
@@ -127,8 +141,8 @@
     for i, (own, full) in enumerate(shards):
         size = own.shape[1]
         part = rows(full, x * size, size)
-        own_right.append(ag_copy(own.at[0], part, 0, i, right))
-        own_left.append(ag_copy(own.at[0], part, 1, i, left))
+        own_right.append(ag_copy(part, part, 0, i, right))
+        own_left.append(ag_copy(part, part, 1, i, left))
         own_right[i].start()
         own_left[i].start()
 
@@ -137,8 +151,26 @@
             line_sem.at[dz, dc], inc=1, device_id=(x, ep(y, z + dz, c + dc)), device_id_type=MESH
         )
 
-    for load in loads:
+    for load in loads[NW:]:
         load.wait()
+
+    deep = gate_own.shape[1]
+
+    def columns(q):
+        return tokens.at[:, pl.ds(pl.multiple_of(q * deep, LANES), deep)]
+
+    src_copies = []
+    for i, xx in enumerate((right, left, across)):
+        for n, (src, dst) in enumerate(((columns(xx), tok_src.at[x]), (expert_ids, ids_all.at[x]))):
+            src_copies.append(
+                pltpu.make_async_remote_copy(
+                    src, dst, src_send.at[i, n], src_recv.at[i, n], device_id=(xx, e), device_id_type=MESH
+                )
+            )
+            src_copies[-1].start()
+    src_local = pltpu.make_async_copy(columns(x), tok_src.at[x], src_own)
+    src_local.start()
+    ids_all[x] = expert_ids[...]
     lane = lax.broadcasted_iota(jnp.int32, (tok_rows, NE), 1)
     hit = jnp.zeros((tok_rows, NE), F32)
     share = jnp.zeros((tok_rows, NE), F32)
@@ -183,6 +215,9 @@
         there = [(dy, dz, dc) for dy in range(NY) if dy + dz + dc]
         return sorted(there, key=lambda k: -hops(k[0], k[1]))
 
+    everyone = [k for dz, dc in ((0, 0), *shifts) for k in line(dz, dc)]
+    everyone = sorted(everyone, key=lambda k: -hops(k[0], k[1]))
+
     def keep(src, dst):
         at = pl.multiple_of(e * slot, slot)
         dst[pl.ds(at, slot), :] = src[pl.ds(at, slot), :]
@@ -210,31 +245,34 @@
         forwards.append(ag_copy(part, part, 3, i, left))
         forwards[-1].start()
 
+    for k in src_copies:
+        k.wait_recv()
+    src_local.wait()
+    for g in range(NX):
+        found = jnp.zeros((tok_rows, NE), F32)
+        for k in range(top):
+            found = found + jnp.where(lane == ids_all[g, :, k : k + 1], 1.0, 0.0)
+        picked = dot(found.astype(BF), tok_src[g], 0, 0)
+        for j in range(per):
+            spread_more[pl.ds(g * per + j, NE, stride=blocks), :] = picked[:, j * LANES : (j + 1) * LANES]
+    more_send[...] = spread_more[...].reshape(NE, blocks, LANES).astype(BF)
+    for dy, dz, dc in everyone:
+        d = ep(y + dy, z + dz, c + dc)
+        pltpu.make_async_remote_copy(
+            more_send.at[d], more_recv.at[e], ext_send, ext_recv, device_id=(x, d), device_id_type=MESH
+        ).start()
+    more_recv[e] = more_send[e]
+
     wait_all(recv, out_recv)
     spread[...] = recv[...].astype(F32)
-    per = blocks // NX
     for j in range(blocks):
         at = slice(j % per * LANES, (j % per + 1) * LANES)
         rows_in[j // per, :, at] = spread[pl.ds(j, NE, stride=slot), :].astype(BF)
 
-    tok_copies = []
-    for i, xx in enumerate((right, left, across)):
-        tok_copies.append(
-            pltpu.make_async_remote_copy(
-                rows_in.at[xx],
-                tok_all.at[x],
-                tok_send.at[i],
-                tok_recv.at[i],
-                device_id=(xx, e),
-                device_id_type=MESH,
-            )
-        )
-        tok_copies[-1].start()
     for j in range(blocks):
         scaled[:, j * LANES : (j + 1) * LANES] = spread[pl.ds(blocks + j, NE, stride=slot), :].astype(BF)
     for f in forwards[:4]:
         f.wait_recv()
-    deep = gate_own.shape[1]
     pre_gate = jnp.zeros((NE, gate_full.shape[1]), F32)
     pre_up = jnp.zeros((NE, gate_full.shape[1]), F32)
     for q in range(NX):
@@ -277,9 +315,6 @@
         copies.append(rs_copy(fwd.at[1], fin.at[1, 1], 5, left))
         copies[-1].start()
 
-    part_down[...] = dot(hidden, scaled[...], 0, 0).astype(BF)
-    down_copies = scatter(part_down, hop_down, fin_down)
-
     for f in forwards[4:]:
         f.wait_recv()
     hidden_grad = dot(scaled[...], down_full[...], 1, 1)
@@ -294,19 +329,35 @@
         )
 
     pre_copies = [pre_copy(pre_all.at[x], 0, right), pre_copy(pre_all.at[x], 1, left)]
+    def give_back(value, first, src, dst, kind):
+        for j in range(blocks):
+            spread[pl.ds(first + j, NE, stride=blocks), :] = value[:, j * LANES : (j + 1) * LANES]
+        src[...] = spread[first : first + NE * blocks, :].reshape(NE, blocks, LANES).astype(BF)
+        for dy, dz, dc in everyone:
+            d = ep(y + dy, z + dz, c + dc)
+            pltpu.make_async_remote_copy(
+                src.at[d],
+                dst.at[e],
+                ret_send.at[kind],
+                ret_recv.at[kind],
+                device_id=(x, d),
+                device_id_type=MESH,
+            ).start()
+        dst[e] = src[e]
+
+    def wait_back(ref, sem):
+        part = ref.at[pl.ds(0, NE - 1)]
+        pltpu.make_async_copy(part, part, sem).wait()
+
+    give_back(dot(hidden, down_full[...]), 0, outs_send, outs_recv, 0)
     for k in pre_copies:
         k.start()
 
-    expert_out = dot(hidden, down_full[...])
-    for j in range(blocks):
-        spread[pl.ds(j, NE, stride=slot), :] = expert_out[:, j * LANES : (j + 1) * LANES]
     slot_grad = dot(gate_pre, gate_full[...], 1, 1) + dot(up_pre, up_full[...], 1, 1)
-    for j in range(blocks):
-        spread[pl.ds(blocks + j, NE, stride=slot), :] = slot_grad[:, j * LANES : (j + 1) * LANES]
-    back_send[...] = spread[...].astype(BF)
-    everyone = [k for dz, dc in ((0, 0), *shifts) for k in line(dz, dc)]
-    exchange(back_send, back_recv, ret_send, ret_recv, sorted(everyone, key=lambda k: -hops(k[0], k[1])))
-    keep(back_send, back_recv)
+    give_back(slot_grad, NE * blocks, grads_send, grads_recv, 1)
+
+    part_down[...] = dot(hidden, scaled[...], 0, 0).astype(BF)
+    down_copies = scatter(part_down, hop_down, fin_down)
 
     pass_on(part_down, hop_down, fwd_down, fin_down, down_copies)
     for kind, xx, source in ((0, right, left), (1, left, right)):
@@ -325,34 +376,46 @@
                 mine.astype(F32) + fin[0, h].astype(F32) + fin[1, h].astype(F32)
             )
 
-    for k in tok_copies:
-        k.wait_recv()
+    part = more_recv.at[pl.ds(0, NE - 1)]
+    pltpu.make_async_copy(part, part, ext_recv).wait()
+    spread_more[...] = more_recv[...].astype(F32).reshape(NE * blocks, LANES)
+    for g in range(NX):
+        for j in range(per):
+            tok_all[g, :, j * LANES : (j + 1) * LANES] = spread_more[
+                pl.ds(g * per + j, NE, stride=blocks), :
+            ].astype(BF)
     sum_gate = dot(rows_in[x], gate_pre, 0, 0)
     sum_up = dot(rows_in[x], up_pre, 0, 0)
     for xx in (left, right):
         sum_gate = sum_gate + dot(tok_all[xx], pre_all[xx, 0], 0, 0)
         sum_up = sum_up + dot(tok_all[xx], pre_all[xx, 1], 0, 0)
     finish(part_down, fin_down, down_grad, down_copies)
+    wait_back(outs_recv, ret_recv.at[0])
+    spread[: NE * blocks, :] = outs_recv[...].astype(F32).reshape(NE * blocks, LANES)
+    high = share.astype(BF)
+    low = (share - high.astype(F32)).astype(BF)
+    for j in range(blocks):
+        part = spread[pl.ds(j, NE, stride=blocks), :].astype(BF)
+        layer_out[:, j * LANES : (j + 1) * LANES] = (dot(high, part) + dot(low, part)).astype(BF)
+
     for k in pre_copies[2:]:
         k.wait_recv()
     gate_grad[0] = sum_gate + dot(tok_all[across], pre_all[across, 0], 0, 0)
     up_grad[0] = sum_up + dot(tok_all[across], pre_all[across, 1], 0, 0)
 
-    wait_all(back_recv, ret_recv)
-    spread[...] = back_recv[...].astype(F32)
-    high = share.astype(BF)
-    low = (share - high.astype(F32)).astype(BF)
+    wait_back(grads_recv, ret_recv.at[1])
+    spread[NE * blocks :, :] = grads_recv[...].astype(F32).reshape(NE * blocks, LANES)
     for j in range(blocks):
-        at = slice(j * LANES, (j + 1) * LANES)
-        outs = spread[pl.ds(j, NE, stride=slot), :].astype(BF)
-        layer_out[:, at] = (dot(high, outs) + dot(low, outs)).astype(BF)
-        grads = spread[pl.ds(blocks + j, NE, stride=slot), :].astype(BF)
-        token_grad[:, at] = dot(pick, grads).astype(BF)
-
-    for k in (*own_right, *own_left, *forwards, *tok_copies, *pre_copies, *down_copies):
+        part = spread[pl.ds(NE * blocks + j, NE, stride=blocks), :].astype(BF)
+        token_grad[:, j * LANES : (j + 1) * LANES] = dot(pick, part).astype(BF)
+
+    for k in (*own_right, *own_left, *forwards, *src_copies, *pre_copies, *down_copies):
         k.wait_send()
     wait_all(send, out_send)
-    wait_all(back_send, ret_send)
+    wait_back(outs_send, ret_send.at[0])
+    wait_back(grads_send, ret_send.at[1])
+    part = more_send.at[pl.ds(0, NE - 1)]
+    pltpu.make_async_copy(part, part, ext_send).wait()
 
 
 def emit(*refs):
@@ -408,10 +471,15 @@
             pltpu.VMEM(expert_ids.shape, jnp.int32),
             pltpu.VMEM(expert_ids.shape, jnp.int32),
             *full,
-            *[pltpu.VMEM(slots, BF)] * 4,
+            *[pltpu.VMEM(slots, BF)] * 2,
+            *[pltpu.VMEM((NE, width // LANES, LANES), BF)] * 4,
             pltpu.VMEM(slots, F32),
             pltpu.VMEM((NX, NE, share), BF),
             pltpu.VMEM((NE, width), BF),
+            pltpu.VMEM((NX, tokens.shape[0], share), BF),
+            pltpu.VMEM((NX, *expert_ids.shape), jnp.int32),
+            *[pltpu.VMEM((NE, width // LANES, LANES), BF)] * 2,
+            pltpu.VMEM((NE * (width // LANES), LANES), F32),
             pltpu.VMEM((NX, NE, share), BF),
             pltpu.VMEM((NX, 2, NE, hidden), BF),
             pltpu.VMEM((hidden, width), BF),
@@ -422,16 +490,19 @@
             pltpu.SemaphoreType.REGULAR((NZ, NC)),
             dma((4, 3)),
             dma((4, 3)),
-            dma((3,)),
-            dma((3,)),
+            dma((3, 2)),
+            dma((3, 2)),
+            dma,
+            dma,
+            dma,
             dma((4,)),
             dma((4,)),
             dma((6,)),
             dma((6,)),
             dma,
             dma,
-            dma,
-            dma,
+            dma((2,)),
+            dma((2,)),
         ],
         compiler_params=pltpu.CompilerParams(
             collective_id=0, has_side_effects=True, vmem_limit_bytes=GRANT

time: 54.9 us -> 54.3 us (0.989)
  Pallas kernels: 54.1 us -> 53.5 us
    pallas_call x1, Pallas kernels: 53.1 us -> 52.5 us  [per_device(): pl.pallas_call(kernel, out_shape=[pltpu.VMEM(tokens.shape, BF), pltpu.VME...]
where the time goes in v5:
time: 54.3 us; the launch traced here: 54.2 us
  Pallas kernels  53.5 us (99%)
  between operations  0.64 us (1%)
    pallas_call x1, Pallas kernels, per_device(): pl.pallas_call(kernel, out_shape=[pltpu.VMEM(tokens.shape, BF), pltpu.VME...  52.5 us

profile of v5, /device:TPU:1, one launch (start us, length us, event | category | flops | bytes accessed | tf_op | source)
XLA Modules:
  0.0 54.2 jit_solution(6600043660786089710)
XLA Ops:
  0.6 52.5 %moe_step.1 = (bf16[8,1024]{1,0:T(8,128)(2,1)S(1)}, bf16[8,1024]{1,0:T(8,128)(2,1)S(1)}, f32[1,256,384]{2,1,0:T(8,128)S(1)}, f32[1,256,384]{2,1,0:T(8,128)S(1)}, f32[1,96,1024]{2,1,0:T(8,128)S(1)}) custom-call(s32[8]{0:T(128)} %ids_hbm.1, s32[16]{0:T(128)} %counts_hbm.1, bf16[8,1024]{1,0:T(8,128)(2,1)} %tokens_hbm.1, bf16[8,1024]{1,0:T(8,128)(2,1)} %cotangent_hbm.1, ...), custom_call_target="tpu_custom_call" | custom-call | tf_op jit(solution)/shard_map/moe_step/pallas_call | solution.py:455
  53.1 1.1 %emit.1 = (bf16[8,1024]{1,0:T(8,128)(2,1)}, bf16[8,1024]{1,0:T(8,128)(2,1)}, f32[1,256,384]{2,1,0:T(8,128)}, f32[1,256,384]{2,1,0:T(8,128)}, f32[1,96,1024]{2,1,0:T(8,128)}) custom-call(bf16[8,1024]{1,0:T(8,128)(2,1)S(1)} %get-tuple-element.10.refs_0_, bf16[8,1024]{1,0:T(8,128)(2,1)S(1)} %get-tuple-element.11.refs_1_, ...), custom_call_target="tpu_custom_call" | custom-call | tf_op jit(solution)/shard_map/emit/pallas_call | solution.py:522

commit v6 on v5

--- a/solution.py
+++ b/solution.py
@@ -390,6 +390,11 @@
         sum_gate = sum_gate + dot(tok_all[xx], pre_all[xx, 0], 0, 0)
         sum_up = sum_up + dot(tok_all[xx], pre_all[xx, 1], 0, 0)
     finish(part_down, fin_down, down_grad, down_copies)
+    for k in pre_copies[2:]:
+        k.wait_recv()
+    gate_grad[0] = sum_gate + dot(tok_all[across], pre_all[across, 0], 0, 0)
+    up_grad[0] = sum_up + dot(tok_all[across], pre_all[across, 1], 0, 0)
+
     wait_back(outs_recv, ret_recv.at[0])
     spread[: NE * blocks, :] = outs_recv[...].astype(F32).reshape(NE * blocks, LANES)
     high = share.astype(BF)
@@ -397,11 +402,6 @@
     for j in range(blocks):
         part = spread[pl.ds(j, NE, stride=blocks), :].astype(BF)
         layer_out[:, j * LANES : (j + 1) * LANES] = (dot(high, part) + dot(low, part)).astype(BF)
-
-    for k in pre_copies[2:]:
-        k.wait_recv()
-    gate_grad[0] = sum_gate + dot(tok_all[across], pre_all[across, 0], 0, 0)
-    up_grad[0] = sum_up + dot(tok_all[across], pre_all[across, 1], 0, 0)
 
     wait_back(grads_recv, ret_recv.at[1])
     spread[NE * blocks :, :] = grads_recv[...].astype(F32).reshape(NE * blocks, LANES)

time: 54.3 us -> 54.3 us (level)
  no operation moved by 1% of the time
where the time goes in v6:
time: 54.3 us; the launch traced here: 54.2 us
  Pallas kernels  53.5 us (99%)
  between operations  0.64 us (1%)
    pallas_call x1, Pallas kernels, per_device(): pl.pallas_call(kernel, out_shape=[pltpu.VMEM(tokens.shape, BF), pltpu.VME...  52.5 us

profile of v6, /device:TPU:1, one launch (start us, length us, event | category | flops | bytes accessed | tf_op | source)
XLA Modules:
  0.0 54.2 jit_solution(12552529679921014698)
XLA Ops:
  0.6 52.5 %moe_step.1 = (bf16[8,1024]{1,0:T(8,128)(2,1)S(1)}, bf16[8,1024]{1,0:T(8,128)(2,1)S(1)}, f32[1,256,384]{2,1,0:T(8,128)S(1)}, f32[1,256,384]{2,1,0:T(8,128)S(1)}, f32[1,96,1024]{2,1,0:T(8,128)S(1)}) custom-call(s32[8]{0:T(128)} %ids_hbm.1, s32[16]{0:T(128)} %counts_hbm.1, bf16[8,1024]{1,0:T(8,128)(2,1)} %tokens_hbm.1, bf16[8,1024]{1,0:T(8,128)(2,1)} %cotangent_hbm.1, ...), custom_call_target="tpu_custom_call" | custom-call | tf_op jit(solution)/shard_map/moe_step/pallas_call | solution.py:455
  53.1 1.1 %emit.1 = (bf16[8,1024]{1,0:T(8,128)(2,1)}, bf16[8,1024]{1,0:T(8,128)(2,1)}, f32[1,256,384]{2,1,0:T(8,128)}, f32[1,256,384]{2,1,0:T(8,128)}, f32[1,96,1024]{2,1,0:T(8,128)}) custom-call(bf16[8,1024]{1,0:T(8,128)(2,1)S(1)} %get-tuple-element.10.refs_0_, bf16[8,1024]{1,0:T(8,128)(2,1)S(1)} %get-tuple-element.11.refs_1_, ...), custom_call_target="tpu_custom_call" | custom-call | tf_op jit(solution)/shard_map/emit/pallas_call | solution.py:522
